TPU v7x, 128 devices: a whole 4x4x4 slice. The times are simulated.
128 devices in a mesh: ep: 64 (over z, y, x), dp: 2 (over core).
Axes of the slice: x: 4, y: 4, z: 4, core: 2. Of those that a mesh axis runs over, the one named last changes fastest.
Arguments:
- act_in: bfloat16 [98304, 448], P(('ep', 'dp'))
- grad_out: bfloat16 [98304, 448], P(('ep', 'dp'))
- slot_ids: int32 [2, 98304, 2], P(None, ('ep', 'dp'))
- gate_vals: float32 [2, 98304, 2], P(None, ('ep', 'dp'))
- w_dense: bfloat16 [2, 448, 448], replicated
- w_gate: bfloat16 [2, 128, 448, 304], P(None, 'ep')
- w_up: bfloat16 [2, 128, 448, 304], P(None, 'ep')
- w_down: bfloat16 [2, 128, 304, 448], P(None, 'ep')
- ws_gate: bfloat16 [2, 448, 304], replicated
- ws_up: bfloat16 [2, 448, 304], replicated
- ws_down: bfloat16 [2, 304, 448], replicated
Outputs:
- output 1: bfloat16 [98304, 448], P(('ep', 'dp'))
- output 2: bfloat16 [2, 448, 448], replicated
- output 3: bfloat16 [2, 128, 448, 304], P(None, 'ep')
- output 4: bfloat16 [2, 128, 448, 304], P(None, 'ep')
- output 5: bfloat16 [2, 128, 304, 448], P(None, 'ep')
- output 6: bfloat16 [2, 448, 304], replicated
- output 7: bfloat16 [2, 448, 304], replicated
- output 8: bfloat16 [2, 304, 448], replicated
All inputs are finite; a program needn't handle non-finite values.
Results may differ from a plain program's by a relative error of at most 0.02.
Values are sent between devices in bfloat16 or wider.
A program may use at most 1 GiB of HBM per device.

v0:
```python
import jax
import jax.numpy as jnp
from jax import lax
from jax.sharding import PartitionSpec as P

ALL_AXES = ("ep", "dp")


def silu_grad(pre_act):
    sigma = jax.nn.sigmoid(pre_act)
    return sigma * (1.0 + pre_act * (1.0 - sigma))


def contract_rows(left, right):
    return lax.dot_general(left, right, (((0,), (0,)), ((), ())), preferred_element_type=jnp.float32)


def contract_cols(left, right):
    return lax.dot_general(left, right, (((1,), (1,)), ((), ())), preferred_element_type=jnp.float32)


def layer_front(act, weights, slot_ids, ep_size):
    w_dense, w_gate, w_up, w_down, ws_gate, ws_up, ws_down = weights
    tokens, width = act.shape
    top = slot_ids.shape[1]
    local_exp = w_gate.shape[0]
    capacity = 2 * tokens * top // (local_exp * ep_size)
    dense_pre = jnp.dot(act, w_dense, preferred_element_type=jnp.float32)
    mixed = (act.astype(jnp.float32) + dense_pre).astype(jnp.bfloat16)
    slot_flat = slot_ids.reshape(tokens * top)
    copy_ids = jnp.arange(1, tokens * top + 1, dtype=jnp.int32)
    slot_owner = jnp.zeros((local_exp * ep_size * capacity,), jnp.int32).at[slot_flat].set(copy_ids)
    tok_owner = (slot_owner + top - 1) // top
    mixed_ext = jnp.concatenate([jnp.zeros((1, width), mixed.dtype), mixed], axis=0)
    send_buf = jnp.take(mixed_ext, tok_owner, axis=0).reshape(ep_size, local_exp, capacity, width)
    recv_rows = lax.all_to_all(send_buf, "ep", 0, 1).reshape(local_exp, ep_size * capacity, width)
    a_one = jnp.einsum("erd,edf->erf", recv_rows, w_gate, preferred_element_type=jnp.float32)
    a_three = jnp.einsum("erd,edf->erf", recv_rows, w_up, preferred_element_type=jnp.float32)
    hidden = (jax.nn.silu(a_one) * a_three).astype(jnp.bfloat16)
    s_one = jnp.dot(mixed, ws_gate, preferred_element_type=jnp.float32)
    s_three = jnp.dot(mixed, ws_up, preferred_element_type=jnp.float32)
    shared_hidden = (jax.nn.silu(s_one) * s_three).astype(jnp.bfloat16)
    return (act, mixed, slot_flat, slot_owner, recv_rows, a_one, a_three, hidden, s_one, s_three, shared_hidden)


def layer_finish(saved, weights, gate_vals, ep_size):
    act, mixed, slot_flat, slot_owner, recv_rows, a_one, a_three, hidden, s_one, s_three, shared_hidden = saved
    w_down = weights[3]
    ws_down = weights[6]
    tokens, width = mixed.shape
    top = gate_vals.shape[1]
    local_exp = hidden.shape[0]
    capacity = recv_rows.shape[1] // ep_size
    exp_out = jnp.einsum("erf,efd->erd", hidden, w_down, preferred_element_type=jnp.float32).astype(jnp.bfloat16)
    back_rows = lax.all_to_all(exp_out.reshape(local_exp, ep_size, capacity, width), "ep", 1, 0).reshape(local_exp * ep_size * capacity, width)
    picked = jnp.take(back_rows, slot_flat, axis=0).reshape(tokens, top, width)
    routed = jnp.sum(gate_vals[:, :, None] * picked.astype(jnp.float32), axis=1)
    shared_out = jnp.dot(shared_hidden, ws_down, preferred_element_type=jnp.float32)
    return (mixed.astype(jnp.float32) + routed + shared_out).astype(jnp.bfloat16)


def layer_backward(grad_y, saved, weights, gate_vals, ep_size):
    act, mixed, slot_flat, slot_owner, recv_rows, a_one, a_three, hidden, s_one, s_three, shared_hidden = saved
    w_dense, w_gate, w_up, w_down, ws_gate, ws_up, ws_down = weights
    tokens, width = grad_y.shape
    top = gate_vals.shape[1]
    local_exp = hidden.shape[0]
    capacity = recv_rows.shape[1] // ep_size
    grad_y32 = grad_y.astype(jnp.float32)
    grad_pick = (gate_vals[:, :, None] * grad_y32[:, None, :]).astype(jnp.bfloat16).reshape(tokens * top, width)
    grad_ext = jnp.concatenate([jnp.zeros((1, width), grad_pick.dtype), grad_pick], axis=0)
    send_grad = jnp.take(grad_ext, slot_owner, axis=0).reshape(ep_size, local_exp, capacity, width)
    grad_exp_out = lax.all_to_all(send_grad, "ep", 0, 1).reshape(local_exp, ep_size * capacity, width)
    g_w_down = jnp.einsum("erf,erd->efd", hidden, grad_exp_out, preferred_element_type=jnp.float32)
    grad_hidden = jnp.einsum("erd,efd->erf", grad_exp_out, w_down, preferred_element_type=jnp.float32)
    grad_a_one = (grad_hidden * a_three * silu_grad(a_one)).astype(jnp.bfloat16)
    grad_a_three = (grad_hidden * jax.nn.silu(a_one)).astype(jnp.bfloat16)
    g_w_gate = jnp.einsum("erd,erf->edf", recv_rows, grad_a_one, preferred_element_type=jnp.float32)
    g_w_up = jnp.einsum("erd,erf->edf", recv_rows, grad_a_three, preferred_element_type=jnp.float32)
    grad_rows = (jnp.einsum("erf,edf->erd", grad_a_one, w_gate, preferred_element_type=jnp.float32) + jnp.einsum("erf,edf->erd", grad_a_three, w_up, preferred_element_type=jnp.float32)).astype(jnp.bfloat16)
    grad_back = lax.all_to_all(grad_rows.reshape(local_exp, ep_size, capacity, width), "ep", 1, 0).reshape(local_exp * ep_size * capacity, width)
    grad_routed = jnp.sum(jnp.take(grad_back, slot_flat, axis=0).reshape(tokens, top, width).astype(jnp.float32), axis=1)
    g_ws_down = contract_rows(shared_hidden, grad_y)
    grad_shared = contract_cols(grad_y, ws_down)
    grad_s_one = (grad_shared * s_three * silu_grad(s_one)).astype(jnp.bfloat16)
    grad_s_three = (grad_shared * jax.nn.silu(s_one)).astype(jnp.bfloat16)
    g_ws_gate = contract_rows(mixed, grad_s_one)
    g_ws_up = contract_rows(mixed, grad_s_three)
    grad_mixed = (grad_y32 + grad_routed + contract_cols(grad_s_one, ws_gate) + contract_cols(grad_s_three, ws_up)).astype(jnp.bfloat16)
    g_w_dense = contract_rows(act, grad_mixed)
    grad_act = (grad_mixed.astype(jnp.float32) + contract_cols(grad_mixed, w_dense)).astype(jnp.bfloat16)
    dense_grads = (g_w_dense.astype(jnp.bfloat16), g_ws_gate.astype(jnp.bfloat16), g_ws_up.astype(jnp.bfloat16), g_ws_down.astype(jnp.bfloat16))
    expert_grads = (g_w_gate.astype(jnp.bfloat16), g_w_up.astype(jnp.bfloat16), g_w_down.astype(jnp.bfloat16))
    return grad_act, dense_grads, expert_grads


def solution(mesh):
    ep_size = mesh.shape["ep"]
    tok_spec = P(ALL_AXES, None)
    route_spec = P(None, ALL_AXES, None)
    exp_spec = P(None, "ep", None, None)
    repl_spec = P(None, None, None)

    def body(act_in, grad_out, slot_ids, gate_vals, w_dense, w_gate, w_up, w_down, ws_gate, ws_up, ws_down):
        layers = w_dense.shape[0]
        all_weights = [(w_dense[layer], w_gate[layer], w_up[layer], w_down[layer], ws_gate[layer], ws_up[layer], ws_down[layer]) for layer in range(layers)]
        saved_all = []
        act = act_in
        for layer in range(layers):
            saved = layer_front(act, all_weights[layer], slot_ids[layer], ep_size)
            saved_all.append(saved)
            if layer + 1 < layers:
                act = layer_finish(saved, all_weights[layer], gate_vals[layer], ep_size)
        grad_act = grad_out
        dense_sums = [None] * layers
        expert_sums = [None] * layers
        for layer in reversed(range(layers)):
            grad_act, dense_grads, expert_grads = layer_backward(grad_act, saved_all[layer], all_weights[layer], gate_vals[layer], ep_size)
            dense_sums[layer] = [lax.psum(part, ALL_AXES) for part in dense_grads]
            expert_sums[layer] = [lax.psum(part, "dp") for part in expert_grads]
        dense_out = [jnp.stack([dense_sums[layer][which] for layer in range(layers)]) for which in range(4)]
        expert_out = [jnp.stack([expert_sums[layer][which] for layer in range(layers)]) for which in range(3)]
        return (grad_act, dense_out[0], expert_out[0], expert_out[1], expert_out[2], dense_out[1], dense_out[2], dense_out[3])

    return jax.shard_map(body, mesh=mesh, in_specs=(tok_spec, tok_spec, route_spec, route_spec, repl_spec, exp_spec, exp_spec, exp_spec, repl_spec, repl_spec, repl_spec), out_specs=(tok_spec, repl_spec, exp_spec, exp_spec, exp_spec, repl_spec, repl_spec, repl_spec), check_vma=False)
```

profile of v0, /device:TPU:1, one launch (start us, length us, event | category | flops | bytes accessed | tf_op | source)
XLA Modules:
  0.0 711.8 jit_solution(1028763041618760492)
XLA Ops:
  8.4 6.2 scatter_custom_fusion.1
  19.2 13.3 %gather_fusion.1 = bf16[3072,448]{1,0:T(8,128)(2,1)} fusion(bf16[769,448]{1,0:T(8,128)(2,1)S(1)} %concatenate.13.clone, s32[3072]{0:T(1024)S(1)} %get-tuple-element.60), kind=kCustom, calls=%fused_computation.1.clone | custom fusion | bytes 5517312 | tf_op jit(solution)/shard_map/jit(_take)/gather | solution.py:35
  32.5 4.1 broadcast_select_fusion.2
  36.6 12.0 %all-to-all-start.1 = ((bf16[64,2,1,24,448]{4,3,1,2,0:T(8,128)(2,1)}), bf16[64,2,1,24,448]{4,3,1,2,0:T(8,128)(2,1)S(1)}, u32[]{:S(2)}, u32[]{:S(2)}) async-start(bf16[64,2,1,24,448]{4,3,1,2,0:T(8,128)(2,1)} %bitcast.222), calls=%async_computation.1 | async-start | bytes 6291456 | tf_op jit(solution)/shard_map/all_to_all | solution.py:36
  50.3 43.2 %all-to-all-done.1 = bf16[64,2,1,24,448]{4,3,1,2,0:T(8,128)(2,1)S(1)} async-done(((bf16[64,2,1,24,448]{4,3,1,2,0:T(8,128)(2,1)}), bf16[64,2,1,24,448]{4,3,1,2,0:T(8,128)(2,1)S(1)}, u32[]{:S(2)}, u32[]{:S(2)}) %all-to-all-start.1) | async-done | bytes 2752544 | tf_op jit(solution)/shard_map/all_to_all | solution.py:36
  109.2 10.4 %all-to-all-start.2 = ((bf16[1,2,64,24,448]{4,3,1,0,2:T(8,128)(2,1)}), bf16[1,2,64,24,448]{4,3,1,0,2:T(8,128)(2,1)}, u32[]{:S(2)}, u32[]{:S(2)}) async-start(bf16[1,2,64,24,448]{4,3,1,0,2:T(8,128)(2,1)} %copy.84), calls=%async_computation.2 | async-start | bytes 6291456 | tf_op jit(solution)/shard_map/all_to_all | solution.py:55
  120.4 6.6 scatter_custom_fusion
  137.1 13.3 %gather_fusion = bf16[3072,448]{1,0:T(8,128)(2,1)} fusion(bf16[1537,448]{1,0:T(8,128)(2,1)S(1)} %concatenate.12, s32[3072]{0:T(1024)S(1)} %get-tuple-element.66), kind=kCustom, calls=%fused_computation.clone | custom fusion | bytes 5517312 | tf_op jit(solution)/shard_map/jit(_take)/gather | solution.py:72
  156.4 9.3 %all-to-all-done.2 = bf16[1,2,64,24,448]{4,3,1,0,2:T(8,128)(2,1)} async-done(((bf16[1,2,64,24,448]{4,3,1,0,2:T(8,128)(2,1)}), bf16[1,2,64,24,448]{4,3,1,0,2:T(8,128)(2,1)}, u32[]{:S(2)}, u32[]{:S(2)}) %all-to-all-start.2) | async-done | bytes 2752544 | tf_op jit(solution)/shard_map/all_to_all | solution.py:55
  165.7 9.3 %all-to-all-start = ((bf16[64,2,1,24,448]{4,3,1,2,0:T(8,128)(2,1)}), bf16[64,2,1,24,448]{4,3,1,2,0:T(8,128)(2,1)}, u32[]{:S(2)}, u32[]{:S(2)}) async-start(bf16[64,2,1,24,448]{4,3,1,2,0:T(8,128)(2,1)} %bitcast.1), calls=%async_computation | async-start | bytes 6291456 | tf_op jit(solution)/shard_map/all_to_all | solution.py:73
  176.0 7.2 %gather_fusion.2 = bf16[1536,448]{1,0:T(8,128)(2,1)S(1)} fusion(bf16[3072,448]{1,0:T(8,128)(2,1)} %bitcast.19, s32[2048]{0:T(1024)S(1)} %pad_clamp_fusion.1), kind=kCustom, calls=%fused_computation.2.clone | custom fusion | bytes 2758656 | tf_op jit(solution)/shard_map/jit(_take)/gather | solution.py:56
  189.0 6.8 multiply_reduce_fusion
  201.5 13.3 %gather_fusion.3 = bf16[3072,448]{1,0:T(8,128)(2,1)} fusion(bf16[769,448]{1,0:T(8,128)(2,1)S(1)} %concatenate.14.clone, s32[3072]{0:T(1024)S(1)} %copy-done.68), kind=kCustom, calls=%fused_computation.4.clone | custom fusion | bytes 5517312 | tf_op jit(solution)/shard_map/jit(_take)/gather | solution.py:35
  214.8 4.2 broadcast_select_fusion.1
  219.1 10.4 %all-to-all-start.3 = ((bf16[64,2,1,24,448]{4,3,1,2,0:T(8,128)(2,1)}), bf16[64,2,1,24,448]{4,3,1,2,0:T(8,128)(2,1)S(1)}, u32[]{:S(2)}, u32[]{:S(2)}) async-start(bf16[64,2,1,24,448]{4,3,1,2,0:T(8,128)(2,1)} %bitcast.25), calls=%async_computation.3 | async-start | bytes 6291456 | tf_op jit(solution)/shard_map/all_to_all | solution.py:36
  233.3 42.3 %all-to-all-done.3 = bf16[64,2,1,24,448]{4,3,1,2,0:T(8,128)(2,1)S(1)} async-done(((bf16[64,2,1,24,448]{4,3,1,2,0:T(8,128)(2,1)}), bf16[64,2,1,24,448]{4,3,1,2,0:T(8,128)(2,1)S(1)}, u32[]{:S(2)}, u32[]{:S(2)}) %all-to-all-start.3) | async-done | bytes 2752544 | tf_op jit(solution)/shard_map/all_to_all | solution.py:36
  296.1 7.8 %all-to-all-start.4 = ((bf16[1,2,64,24,448]{4,3,1,0,2:T(8,128)(2,1)}), bf16[1,2,64,24,448]{4,3,1,0,2:T(8,128)(2,1)S(1)}, u32[]{:S(2)}, u32[]{:S(2)}) async-start(bf16[1,2,64,24,448]{4,3,1,0,2:T(8,128)(2,1)} %copy.92), calls=%async_computation.4 | async-start | bytes 6291456 | tf_op jit(solution)/shard_map/all_to_all | solution.py:81
  312.0 36.5 %all-to-all-done.4 = bf16[1,2,64,24,448]{4,3,1,0,2:T(8,128)(2,1)S(1)} async-done(((bf16[1,2,64,24,448]{4,3,1,0,2:T(8,128)(2,1)}), bf16[1,2,64,24,448]{4,3,1,0,2:T(8,128)(2,1)S(1)}, u32[]{:S(2)}, u32[]{:S(2)}) %all-to-all-start.4) | async-done | bytes 2752544 | tf_op jit(solution)/shard_map/all_to_all | solution.py:81
  348.6 5.4 gather_fusion.4
  359.1 5.7 reduce_sum.28
  372.8 4.4 mul.163
  377.9 13.3 %gather_fusion.5 = bf16[3072,448]{1,0:T(8,128)(2,1)} fusion(bf16[1537,448]{1,0:T(8,128)(2,1)S(1)} %concatenate.15, s32[3072]{0:T(1024)S(1)} %copy-done.67), kind=kCustom, calls=%fused_computation.3.clone | custom fusion | bytes 5517312 | tf_op jit(solution)/shard_map/jit(_take)/gather | solution.py:72
  391.2 4.1 broadcast_select_fusion
  395.3 10.7 %all-to-all-start.5 = ((bf16[64,2,1,24,448]{4,3,1,2,0:T(8,128)(2,1)}), bf16[64,2,1,24,448]{4,3,1,2,0:T(8,128)(2,1)}, u32[]{:S(2)}, u32[]{:S(2)}) async-start(bf16[64,2,1,24,448]{4,3,1,2,0:T(8,128)(2,1)} %bitcast.221), calls=%async_computation.5 | async-start | bytes 6291456 | tf_op jit(solution)/shard_map/all_to_all | solution.py:73
  415.3 36.2 %all-to-all-done.5 = bf16[64,2,1,24,448]{4,3,1,2,0:T(8,128)(2,1)} async-done(((bf16[64,2,1,24,448]{4,3,1,2,0:T(8,128)(2,1)}), bf16[64,2,1,24,448]{4,3,1,2,0:T(8,128)(2,1)}, u32[]{:S(2)}, u32[]{:S(2)}) %all-to-all-start.5) | async-done | bytes 2752544 | tf_op jit(solution)/shard_map/all_to_all | solution.py:73
  455.1 4.0 multiply_convert_fusion.1
  469.9 8.5 %all-to-all-start.6 = ((bf16[1,2,64,24,448]{4,3,1,0,2:T(8,128)(2,1)}), bf16[1,2,64,24,448]{4,3,1,0,2:T(8,128)(2,1)S(1)}, u32[]{:S(2)}, u32[]{:S(2)}) async-start(bf16[1,2,64,24,448]{4,3,1,0,2:T(8,128)(2,1)} %copy.100), calls=%async_computation.6 | async-start | bytes 6291456 | tf_op jit(solution)/shard_map/all_to_all | solution.py:81
  478.4 4.6 fusion.11
  501.0 24.5 %all-to-all-done.6 = bf16[1,2,64,24,448]{4,3,1,0,2:T(8,128)(2,1)S(1)} async-done(((bf16[1,2,64,24,448]{4,3,1,0,2:T(8,128)(2,1)}), bf16[1,2,64,24,448]{4,3,1,0,2:T(8,128)(2,1)S(1)}, u32[]{:S(2)}, u32[]{:S(2)}) %all-to-all-start.6) | async-done | bytes 2752544 | tf_op jit(solution)/shard_map/all_to_all | solution.py:81
  525.5 5.4 gather_fusion.6
  536.0 5.7 reduce_sum.29
  553.3 146.7 %all-reduce.9.cloned.1.call-done = (bf16[1,448,448]{1,2,0:T(8,128)(2,1)}, bf16[1,448,448]{1,2,0:T(8,128)(2,1)}, bf16[1,448,304]{1,2,0:T(8,128)(2,1)}, bf16[1,448...) async-done(((bf16[1,448,448]{1,2,0:T(8,128)(2,1)}, ...) | async-done | bytes 2437136 | tf_op jit(solution)/shard_map/psum | solution.py:119
  (271 shorter events, 161.3 us)
Async XLA Ops:
  7.2 8.0 %copy-start.75 = (s32[1536]{0:T(1024)}, s32[1536]{0:T(1024)S(1)}, u32[]{:S(2)}) copy-start(s32[1536]{0:T(1024)S(1)} %iota_add_fusion) | copy-start | bytes 18436
  8.1 7.1 copy-start.19
  36.6 56.9 %all-to-all-start.1 = ((bf16[64,2,1,24,448]{4,3,1,2,0:T(8,128)(2,1)}), bf16[64,2,1,24,448]{4,3,1,2,0:T(8,128)(2,1)S(1)}, u32[]{:S(2)}, u32[]{:S(2)}) async-start(bf16[64,2,1,24,448]{4,3,1,2,0:T(8,128)(2,1)} %bitcast.222), calls=%async_computation.1 | async-start | bytes 6291456 | tf_op jit(solution)/shard_map/all_to_all | solution.py:36
  109.2 10.4 %copy-start.20 = (s32[1,768,2]{2,1,0:T(8,128)S(1)}, s32[1,768,2]{2,1,0:T(8,128)}, u32[]{:S(2)}) copy-start(s32[1,768,2]{2,1,0:T(8,128)} %copy-done.19) | copy-start | bytes 18436
  109.2 17.8 %copy-start.71 = (f32[1,768,2]{1,2,0:T(2,128)S(1)}, f32[1,768,2]{1,2,0:T(2,128)}, u32[]{:S(2)}) copy-start(f32[1,768,2]{1,2,0:T(2,128)} %get-tuple-element.63) | copy-start | bytes 18436
  109.2 18.8 %copy-start.27 = (bf16[768,448]{0,1:T(8,128)(2,1)S(1)}, bf16[768,448]{0,1:T(8,128)(2,1)}, u32[]{:S(2)}) copy-start(bf16[768,448]{0,1:T(8,128)(2,1)} %param.18) | copy-start | bytes 2064388
  109.2 56.5 %all-to-all-start.2 = ((bf16[1,2,64,24,448]{4,3,1,0,2:T(8,128)(2,1)}), bf16[1,2,64,24,448]{4,3,1,0,2:T(8,128)(2,1)}, u32[]{:S(2)}, u32[]{:S(2)}) async-start(bf16[1,2,64,24,448]{4,3,1,0,2:T(8,128)(2,1)} %copy.84), calls=%async_computation.2 | async-start | bytes 6291456 | tf_op jit(solution)/shard_map/all_to_all | solution.py:55
  137.1 13.3 %copy-start.66 = (s32[1536]{0:T(1024)S(1)}, s32[1536]{0:T(1024)}, u32[]{:S(2)}) copy-start(s32[1536]{0:T(1024)} %reshape_squeeze.36) | copy-start | bytes 18436
  137.1 13.3 %copy-start.6 = (bf16[768,448]{0,1:T(8,128)(2,1)S(1)}, bf16[768,448]{0,1:T(8,128)(2,1)}, u32[]{:S(2)}) copy-start(bf16[768,448]{0,1:T(8,128)(2,1)} %copy-done.5) | copy-start | bytes 2064388
  137.1 13.3 %copy-start.31 = (bf16[2,448,304]{1,2,0:T(8,128)(2,1)S(1)}, bf16[2,448,304]{1,2,0:T(8,128)(2,1)}, u32[]{:S(2)}) copy-start(bf16[2,448,304]{1,2,0:T(8,128)(2,1)} %param.25) | copy-start | bytes 1634308
  165.7 9.3 %copy-start.70 = (f32[768,2]{0,1:T(2,128)S(1)}, f32[768,2]{0,1:T(2,128)}, u32[]{:S(2)}) copy-start(f32[768,2]{0,1:T(2,128)} %get-tuple-element.62) | copy-start | bytes 18436
  165.7 53.3 %all-to-all-start = ((bf16[64,2,1,24,448]{4,3,1,2,0:T(8,128)(2,1)}), bf16[64,2,1,24,448]{4,3,1,2,0:T(8,128)(2,1)}, u32[]{:S(2)}, u32[]{:S(2)}) async-start(bf16[64,2,1,24,448]{4,3,1,2,0:T(8,128)(2,1)} %bitcast.1), calls=%async_computation | async-start | bytes 6291456 | tf_op jit(solution)/shard_map/all_to_all | solution.py:73
  176.0 7.2 %copy-start.72 = (pred[1536]{0:T(1024)(128)(4,1)}, pred[1536]{0:T(1024)(128)(4,1)S(1)}, u32[]{:S(2)}) copy-start(pred[1536]{0:T(1024)(128)(4,1)S(1)} %compare_and_fusion.5) | copy-start | bytes 4612
  199.6 15.3 %copy-start.45 = (bf16[768,448]{0,1:T(8,128)(2,1)}, bf16[768,448]{0,1:T(8,128)(2,1)S(1)}, u32[]{:S(2)}) copy-start(bf16[768,448]{0,1:T(8,128)(2,1)S(1)} %fusion.5) | copy-start | bytes 2064388
  219.1 56.5 %all-to-all-start.3 = ((bf16[64,2,1,24,448]{4,3,1,2,0:T(8,128)(2,1)}), bf16[64,2,1,24,448]{4,3,1,2,0:T(8,128)(2,1)S(1)}, u32[]{:S(2)}, u32[]{:S(2)}) async-start(bf16[64,2,1,24,448]{4,3,1,2,0:T(8,128)(2,1)} %bitcast.25), calls=%async_computation.3 | async-start | bytes 6291456 | tf_op jit(solution)/shard_map/all_to_all | solution.py:36
  278.4 4.9 copy-start.56
  279.6 6.2 copy-start.17
  296.1 52.5 %all-to-all-start.4 = ((bf16[1,2,64,24,448]{4,3,1,0,2:T(8,128)(2,1)}), bf16[1,2,64,24,448]{4,3,1,0,2:T(8,128)(2,1)S(1)}, u32[]{:S(2)}, u32[]{:S(2)}) async-start(bf16[1,2,64,24,448]{4,3,1,0,2:T(8,128)(2,1)} %copy.92), calls=%async_computation.4 | async-start | bytes 6291456 | tf_op jit(solution)/shard_map/all_to_all | solution.py:81
  305.8 4.6 copy-start.64
  359.1 6.2 copy-start.50
  377.9 13.3 %copy-start.74 = (pred[3072]{0:T(1024)(128)(4,1)S(1)}, pred[3072]{0:T(1024)(128)(4,1)}, u32[]{:S(2)}) copy-start(pred[3072]{0:T(1024)(128)(4,1)} %get-tuple-element.57) | copy-start | bytes 9220
  395.3 10.7 %copy-start.1 = (bf16[1,2,64,1,24,448]{5,4,2,1,3,0:T(8,128)(2,1)S(1)}, bf16[1,2,64,1,24,448]{5,4,2,1,3,0:T(8,128)(2,1)}, u32[]{:S(2)}) copy-start(bf16[1,2,64,1,24,448]{5,4,2,1,3,0:T(8,128)(2,1)} %copy-done) | copy-start | bytes 8257540
  395.3 56.1 %all-to-all-start.5 = ((bf16[64,2,1,24,448]{4,3,1,2,0:T(8,128)(2,1)}), bf16[64,2,1,24,448]{4,3,1,2,0:T(8,128)(2,1)}, u32[]{:S(2)}, u32[]{:S(2)}) async-start(bf16[64,2,1,24,448]{4,3,1,2,0:T(8,128)(2,1)} %bitcast.221), calls=%async_computation.5 | async-start | bytes 6291456 | tf_op jit(solution)/shard_map/all_to_all | solution.py:73
  406.0 7.3 %copy-start.18 = (f32[2,1536,304]{1,2,0:T(8,128)S(1)}, f32[2,1536,304]{1,2,0:T(8,128)}, u32[]{:S(2)}) copy-start(f32[2,1536,304]{1,2,0:T(8,128)} %copy-done.17) | copy-start | bytes 11206660
  406.0 7.2 %copy-start.22 = (bf16[1,2,64,1,24,448]{5,4,2,1,3,0:T(8,128)(2,1)S(1)}, bf16[1,2,64,1,24,448]{5,4,2,1,3,0:T(8,128)(2,1)}, u32[]{:S(2)}) copy-start(bf16[1,2,64,1,24,448]{5,4,2,1,3,0:T(8,128)(2,1)} %copy.73) | copy-start | bytes 8257540
  453.7 5.4 copy-start.23
  469.9 55.6 %all-to-all-start.6 = ((bf16[1,2,64,24,448]{4,3,1,0,2:T(8,128)(2,1)}), bf16[1,2,64,24,448]{4,3,1,0,2:T(8,128)(2,1)S(1)}, u32[]{:S(2)}, u32[]{:S(2)}) async-start(bf16[1,2,64,24,448]{4,3,1,0,2:T(8,128)(2,1)} %copy.100), calls=%async_computation.6 | async-start | bytes 6291456 | tf_op jit(solution)/shard_map/all_to_all | solution.py:81
  478.3 69.2 %all-reduce.11.cloned.1.call-start = ((), (), s32[]{:S(2)}) async-start(), calls=%async_computation.8 | async-start | bytes 7471104 | tf_op jit(solution)/shard_map/psum | solution.py:120
  487.0 213.1 %all-reduce.9.cloned.1.call-start = ((), (), s32[]{:S(2)}) async-start(), calls=%async_computation.7 | async-start | bytes 5570560 | tf_op jit(solution)/shard_map/psum | solution.py:119
  489.5 5.5 copy-start.30
  489.5 5.5 copy-start.49
  525.5 5.4 copy-start.73
  (58 other events, 149.3 us)
Sparse Core Ops, SparseCore 0:
  487.1 30.3 all-reduce.10
  546.2 153.7 all-reduce.8
where the time goes:
time: 719 us; the launch traced here: 712 us
  waiting for transfers between devices  339 us (47%)
  local copies, waits for them, and re-layouts  159 us (22%)
  matrix products  78 us (11%)
  starting transfers between devices  69.1 us (10%)
  other arithmetic  51.2 us (7%)
  between operations  15.3 us (2%)
    psum x1, waiting for transfers between devices, body(): dense_sums[layer] = [lax.psum(part, ALL_AXES) for part in dense_grads]  147 us
    all_to_all x2, waiting for transfers between devices, layer_front(): lax.all_to_all(send_buf, 'ep', 0, 1)  85.5 us
    all_to_all x2, waiting for transfers between devices, layer_backward(): lax.all_to_all(grad_rows.reshape(local_exp, ep_size, capacity, width), 'e...  61.1 us
    all_to_all x2, waiting for transfers between devices, layer_backward(): lax.all_to_all(send_grad, 'ep', 0, 1)  36.2 us
    gather x2, local copies, waits for them, and re-layouts, layer_front(): jnp.take(mixed_ext, tok_owner, axis=0)  26.6 us
    gather x2, local copies, waits for them, and re-layouts, layer_backward(): jnp.take(grad_ext, slot_owner, axis=0)  26.6 us
    all_to_all x2, starting transfers between devices, layer_front(): lax.all_to_all(send_buf, 'ep', 0, 1)  22.3 us
    all_to_all x2, starting transfers between devices, layer_backward(): lax.all_to_all(send_grad, 'ep', 0, 1)  19.9 us
  transfers between devices with their start and end apart: 9, of which 7 were waited for; matrix products, arithmetic and copies ran while one was open for 21% of the time, Pallas kernels for 0%

commit v1 on v0

v1 whole, which is shorter than its diff:
```python
import functools
import jax
import jax.numpy as jnp
import numpy as np
from jax import lax
from jax.experimental import pallas as pl
from jax.experimental.pallas import tpu as pltpu
from jax.sharding import PartitionSpec as P

ALL_AXES = ("ep", "dp")
MESH = pl.DeviceIdType.MESH
LANE = 128
VMEM_LIMIT = 60 * 1024 * 1024
F32 = jnp.float32
BF16 = jnp.bfloat16


def pad_lanes(n):
    return (n + LANE - 1) // LANE * LANE


def dot(a, b):
    return lax.dot_general(a, b, (((1,), (0,)), ((), ())), preferred_element_type=F32)


def dot_rows(a, b):
    return lax.dot_general(a, b, (((0,), (0,)), ((), ())), preferred_element_type=F32)


def dot_cols(a, b):
    return lax.dot_general(a, b, (((1,), (1,)), ((), ())), preferred_element_type=F32)


def onehot(cond):
    return jnp.where(cond, 1.0, 0.0).astype(BF16)


def silu(x):
    return x * jax.nn.sigmoid(x)


def silu_grad(x):
    sigma = jax.nn.sigmoid(x)
    return sigma * (1.0 + x * (1.0 - sigma))


def roll_up(x, by):
    return pltpu.roll(x.astype(F32), by, 1)


def join(first, second):
    wide = first.shape[1]
    return jnp.concatenate([first[:, : wide - LANE], first[:, wide - LANE :] + second[:, :LANE], second[:, LANE:]], axis=1)


def spread(lo_ref, hi_ref, rows, at):
    width = rows.shape[1]
    wide = lo_ref.shape[1]
    count = rows.shape[0]
    lo_ref[at : at + count, :] = jnp.zeros((count, wide), BF16)
    lo_ref[at : at + count, :width] = rows
    hi_ref[at : at + count, :] = roll_up(lo_ref[at : at + count, :], wide - width).astype(BF16)


def fill_send(slot_rows, lo_ref, hi_ref, send_ref, per_copy):
    ep, cap, _ = send_ref.shape
    tokens = slot_rows.shape[1]
    step_size = 8
    row0 = slot_rows[0:1, :]
    row1 = slot_rows[1:2, :]

    def body(step, carry):
        shape = (step_size, cap, tokens)
        slot = (lax.broadcasted_iota(jnp.int32, shape, 0) + step * step_size) * (2 * cap) + lax.broadcasted_iota(jnp.int32, shape, 1)
        slot = slot.reshape(step_size * cap, tokens)

        def pick(s):
            if per_copy:
                return jnp.concatenate([onehot(row0 == s), onehot(row1 == s)], axis=1)
            return onehot((row0 == s) | (row1 == s))

        first = dot(pick(slot), lo_ref[...])
        second = dot(pick(slot + cap), hi_ref[...])
        send_ref[pl.ds(step * step_size, step_size)] = join(first, second).astype(BF16).reshape(step_size, cap, send_ref.shape[2])
        return carry

    lax.fori_loop(0, ep // step_size, body, 0)


def halves(ref, width, start=None, size=None):
    ep, cap, full = ref.shape
    wide = pad_lanes(width)
    block = ref[...] if start is None else ref[pl.ds(start, size)]
    block = block.reshape(block.shape[0] * cap, full)
    return block[:, :wide], block[:, full - wide :]


def collect(back_ref, slot_cols, slots_of_row, gate_cols, width, start, count):
    cap = back_ref.shape[1]
    first, second = halves(back_ref, width)
    cols = slot_cols[start : start + count, :]
    col0 = cols[:, 0:1]
    col1 = cols[:, 1:2]
    if gate_cols is None:
        acc0 = dot(onehot((col0 == slots_of_row) | (col1 == slots_of_row)), first)
        acc1 = dot(onehot((col0 == slots_of_row + cap) | (col1 == slots_of_row + cap)), second)
    else:
        gates = gate_cols[start : start + count, :]
        acc0 = gates[:, 0:1] * dot(onehot(col0 == slots_of_row), first) + gates[:, 1:2] * dot(onehot(col1 == slots_of_row), first)
        acc1 = gates[:, 0:1] * dot(onehot(col0 == slots_of_row + cap), second) + gates[:, 1:2] * dot(onehot(col1 == slots_of_row + cap), second)
    return (acc0 + roll_up(acc1, width))[:, :width]


def load_experts(gate_ref, up_ref, down_ref, w13_ref, w2_ref):
    width, ff = gate_ref.shape[1], gate_ref.shape[2]
    wide = w13_ref.shape[1]
    half = w13_ref.shape[2] // 2
    w13_ref[...] = jnp.zeros(w13_ref.shape, BF16)
    w2_ref[...] = jnp.zeros(w2_ref.shape, BF16)
    for e in range(2):
        at = e * (wide - width)
        w13_ref[e, at : at + width, :ff] = gate_ref[e]
        w13_ref[e, at : at + width, half : half + ff] = up_ref[e]
        w2_ref[e, :ff, :width] = down_ref[e]
    w2_ref[1] = roll_up(w2_ref[1], wide - width).astype(BF16)


STEP_DEV = 16


def experts_forward(recv_ref, w13_ref, w2_ref, send_ref, width):
    ep, cap, full = recv_ref.shape
    half = w13_ref.shape[2] // 2

    def body(step, carry):
        rows = halves(recv_ref, width, step * STEP_DEV, STEP_DEV)
        outs = []
        for e in range(2):
            pre = dot(rows[e], w13_ref[e])
            hidden = (silu(pre[:, :half]) * pre[:, half:]).astype(BF16)
            outs.append(dot(hidden, w2_ref[e]))
        send_ref[pl.ds(step * STEP_DEV, STEP_DEV)] = join(outs[0], outs[1]).astype(BF16).reshape(STEP_DEV, cap, full)
        return carry

    lax.fori_loop(0, ep // STEP_DEV, body, 0)


def experts_backward(recv_ref, grad_ref, w13_ref, w2_ref, send_ref, acc13_ref, acc2_ref, width):
    ep, cap, full = recv_ref.shape
    half = w13_ref.shape[2] // 2
    acc13_ref[...] = jnp.zeros(acc13_ref.shape, F32)
    acc2_ref[...] = jnp.zeros(acc2_ref.shape, F32)

    def body(step, carry):
        rows = halves(recv_ref, width, step * STEP_DEV, STEP_DEV)
        grads = halves(grad_ref, width, step * STEP_DEV, STEP_DEV)
        outs = []
        for e in range(2):
            pre = dot(rows[e], w13_ref[e])
            one, three = pre[:, :half], pre[:, half:]
            act = silu(one)
            hidden = (act * three).astype(BF16)
            grad_hidden = dot_cols(grads[e], w2_ref[e])
            grad_one = (grad_hidden * three * silu_grad(one)).astype(BF16)
            grad_three = (grad_hidden * act).astype(BF16)
            grad_pre = jnp.concatenate([grad_one, grad_three], axis=1)
            outs.append(dot_cols(grad_pre, w13_ref[e]))
            acc13_ref[e] += dot_rows(rows[e], grad_pre)
            acc2_ref[e] += dot_rows(hidden, grads[e])
        send_ref[pl.ds(step * STEP_DEV, STEP_DEV)] = join(outs[0], outs[1]).astype(BF16).reshape(STEP_DEV, cap, full)
        return carry

    lax.fori_loop(0, ep // STEP_DEV, body, 0)


def store_expert_grads(acc13_ref, acc2_ref, gate_out, up_out, down_out):
    width, ff = gate_out.shape[1], gate_out.shape[2]
    wide = acc13_ref.shape[1]
    half = acc13_ref.shape[2] // 2
    for e in range(2):
        at = e * (wide - width)
        gate_out[e] = acc13_ref[e, at : at + width, :ff].astype(BF16)
        up_out[e] = acc13_ref[e, at : at + width, half : half + ff].astype(BF16)
        down = acc2_ref[e]
        if e:
            down = roll_up(down, width)
        down_out[e] = down[:ff, :width].astype(BF16)


def dense_front(x, w_dense_ref):
    return (x.astype(F32) + dot(x, w_dense_ref[...])).astype(BF16)


def signal_peers(ep):
    barrier = pltpu.get_barrier_semaphore()
    me = lax.axis_index("ep")

    def body(i, carry):
        pl.semaphore_signal(barrier, inc=1, device_id={"ep": lax.rem(me + i, ep)}, device_id_type=MESH)
        return carry

    lax.fori_loop(1, ep, body, 0)


def wait_peers(ep):
    pl.semaphore_wait(pltpu.get_barrier_semaphore(), ep - 1)


def peer_of(i, ep):
    me = lax.axis_index("ep")
    turn = lax.rem(i - 1 + (ep // 2) * lax.axis_index("dp"), ep - 1) + 1
    return lax.rem(me + turn, ep)


def start_exchange(send_ref, recv_ref, send_sem, recv_sem, local_sem):
    ep = send_ref.shape[0]
    me = lax.axis_index("ep")

    def body(i, carry):
        peer = peer_of(i, ep)
        pltpu.make_async_remote_copy(
            src_ref=send_ref.at[peer],
            dst_ref=recv_ref.at[me],
            send_sem=send_sem.at[peer],
            recv_sem=recv_sem.at[me],
            device_id={"ep": peer},
            device_id_type=MESH,
        ).start()
        return carry

    lax.fori_loop(1, ep, body, 0)
    pltpu.make_async_copy(send_ref.at[me], recv_ref.at[me], local_sem).start()


def finish_exchange(send_ref, recv_ref, send_sem, recv_sem, local_sem):
    ep = send_ref.shape[0]
    me = lax.axis_index("ep")
    pltpu.make_async_copy(send_ref.at[me], recv_ref.at[me], local_sem).wait()

    def body(i, carry):
        peer = lax.rem(me + i, ep)
        copy = pltpu.make_async_remote_copy(
            src_ref=send_ref.at[peer],
            dst_ref=recv_ref.at[peer],
            send_sem=send_sem.at[peer],
            recv_sem=recv_sem.at[peer],
            device_id={"ep": peer},
            device_id_type=MESH,
        )
        copy.wait_send()
        copy.wait_recv()
        return carry

    lax.fori_loop(1, ep, body, 0)


def vmem():
    return pl.BlockSpec(memory_space=pltpu.VMEM)


def call(kernel, ins, outs, scratch, collective_id=None):
    return pl.pallas_call(
        kernel,
        out_shape=outs,
        in_specs=[vmem() for _ in ins],
        out_specs=tuple(vmem() for _ in outs),
        scratch_shapes=scratch,
        compiler_params=pltpu.CompilerParams(collective_id=collective_id, has_side_effects=collective_id is not None, vmem_limit_bytes=VMEM_LIMIT),
    )(*ins)


def exchange_scratch(ep):
    return [pltpu.SemaphoreType.DMA((ep,)), pltpu.SemaphoreType.DMA((ep,)), pltpu.SemaphoreType.DMA]


def shape(dims, dtype=BF16):
    return jax.ShapeDtypeStruct(dims, dtype)


def dispatch_kernel(x_ref, wd_ref, slot_row_ref, u_ref, recv_ref, send_ref, lo_ref, hi_ref, *sems):
    ep = recv_ref.shape[0]
    signal_peers(ep)
    u = dense_front(x_ref[...], wd_ref)
    u_ref[...] = u
    spread(lo_ref, hi_ref, u, 0)
    fill_send(slot_row_ref[...], lo_ref, hi_ref, send_ref, False)
    wait_peers(ep)
    start_exchange(send_ref, recv_ref, *sems)
    finish_exchange(send_ref, recv_ref, *sems)


def forward_kernel(rows_ref, gate_ref, up_ref, down_ref, recv_ref, send_ref, w13_ref, w2_ref, *sems):
    ep = recv_ref.shape[0]
    signal_peers(ep)
    load_experts(gate_ref, up_ref, down_ref, w13_ref, w2_ref)
    experts_forward(rows_ref, w13_ref, w2_ref, send_ref, gate_ref.shape[1])
    wait_peers(ep)
    start_exchange(send_ref, recv_ref, *sems)
    finish_exchange(send_ref, recv_ref, *sems)


def shared_out(u, s1_ref, s3_ref, s2_ref):
    one = dot(u, s1_ref[...])
    three = dot(u, s3_ref[...])
    return dot((silu(one) * three).astype(BF16), s2_ref[...])


def between_kernel(back_ref, slots_of_row_ref, slot_col_ref, gate_col_ref, u_ref, s1_ref, s3_ref, s2_ref, wd_ref, slot_row_ref, x_out_ref, u_out_ref, recv_ref, send_ref, lo_ref, hi_ref, *sems):
    ep = recv_ref.shape[0]
    tokens, width = u_ref.shape
    signal_peers(ep)
    count = 256
    for start in range(0, tokens, count):
        u = u_ref[start : start + count, :]
        routed = collect(back_ref, slot_col_ref, slots_of_row_ref[...], gate_col_ref, width, start, count)
        x = (u.astype(F32) + routed + shared_out(u, s1_ref, s3_ref, s2_ref)).astype(BF16)
        x_out_ref[start : start + count, :] = x
        mixed = dense_front(x, wd_ref)
        u_out_ref[start : start + count, :] = mixed
        spread(lo_ref, hi_ref, mixed, start)
    fill_send(slot_row_ref[...], lo_ref, hi_ref, send_ref, False)
    wait_peers(ep)
    start_exchange(send_ref, recv_ref, *sems)
    finish_exchange(send_ref, recv_ref, *sems)


def spread_gated(grad, gate_col_ref, lo_ref, hi_ref, start):
    tokens = gate_col_ref.shape[0]
    count = grad.shape[0]
    gates = gate_col_ref[start : start + count, :]
    for j in range(2):
        spread(lo_ref, hi_ref, (gates[:, j : j + 1] * grad.astype(F32)).astype(BF16), j * tokens + start)


def grad_dispatch_kernel(grad_ref, gate_col_ref, slot_row_ref, recv_ref, send_ref, lo_ref, hi_ref, *sems):
    ep = recv_ref.shape[0]
    signal_peers(ep)
    spread_gated(grad_ref[...], gate_col_ref, lo_ref, hi_ref, 0)
    fill_send(slot_row_ref[...], lo_ref, hi_ref, send_ref, True)
    wait_peers(ep)
    start_exchange(send_ref, recv_ref, *sems)
    finish_exchange(send_ref, recv_ref, *sems)


def backward_kernel(rows_ref, grads_ref, gate_ref, up_ref, down_ref, recv_ref, g_gate_ref, g_up_ref, g_down_ref, send_ref, w13_ref, w2_ref, acc13_ref, acc2_ref, *sems):
    ep = recv_ref.shape[0]
    signal_peers(ep)
    load_experts(gate_ref, up_ref, down_ref, w13_ref, w2_ref)
    experts_backward(rows_ref, grads_ref, w13_ref, w2_ref, send_ref, acc13_ref, acc2_ref, gate_ref.shape[1])
    wait_peers(ep)
    start_exchange(send_ref, recv_ref, *sems)
    store_expert_grads(acc13_ref, acc2_ref, g_gate_ref, g_up_ref, g_down_ref)
    finish_exchange(send_ref, recv_ref, *sems)


def shared_backward(grad, u, s1_ref, s3_ref, s2_ref, pack_ref, width, ff):
    one = dot(u, s1_ref[...])
    three = dot(u, s3_ref[...])
    act = silu(one)
    hidden = (act * three).astype(BF16)
    grad_hidden = dot_cols(grad, s2_ref[...])
    grad_one = (grad_hidden * three * silu_grad(one)).astype(BF16)
    grad_three = (grad_hidden * act).astype(BF16)
    at = pad_lanes(width)
    pack_ref[...] = jnp.zeros(pack_ref.shape, BF16)
    for part in (dot_rows(u, grad_one), dot_rows(u, grad_three), dot_rows(grad, hidden)):
        pack_ref[:, at : at + ff] = part.astype(BF16)
        at += pad_lanes(ff)
    return dot_cols(grad_one, s1_ref[...]) + dot_cols(grad_three, s3_ref[...])


def back_to_tokens(back_ref, slots_of_row_ref, slot_col_ref, grad_ref, u_ref, x_ref, s1_ref, s3_ref, s2_ref, wd_ref, pack_ref, mixed_ref, shared_ref, grad_x_ref):
    tokens, width = u_ref.shape
    ff = s1_ref.shape[1]
    shared_ref[...] = shared_backward(grad_ref[...], u_ref[...], s1_ref, s3_ref, s2_ref, pack_ref, width, ff)
    count = 256
    for start in range(0, tokens, count):
        rows = slice(start, start + count)
        routed = collect(back_ref, slot_col_ref, slots_of_row_ref[...], None, width, start, count)
        mixed = (grad_ref[rows, :].astype(F32) + routed + shared_ref[rows, :]).astype(BF16)
        mixed_ref[rows, :] = mixed
        grad_x_ref[rows, :] = (mixed.astype(F32) + dot_cols(mixed, wd_ref[...])).astype(BF16)
    pack_ref[:, :width] = dot_rows(x_ref[...], mixed_ref[...]).astype(BF16)


def turn_kernel(back_ref, slots_of_row_ref, slot_col_ref, grad_ref, u_ref, x_ref, s1_ref, s3_ref, s2_ref, wd_ref, gate_col_ref, slot_row_ref, grad_x_ref, pack_ref, recv_ref, send_ref, lo_ref, hi_ref, mixed_ref, shared_ref, *sems):
    ep = recv_ref.shape[0]
    signal_peers(ep)
    back_to_tokens(back_ref, slots_of_row_ref, slot_col_ref, grad_ref, u_ref, x_ref, s1_ref, s3_ref, s2_ref, wd_ref, pack_ref, mixed_ref, shared_ref, grad_x_ref)
    spread_gated(grad_x_ref[...], gate_col_ref, lo_ref, hi_ref, 0)
    fill_send(slot_row_ref[...], lo_ref, hi_ref, send_ref, True)
    wait_peers(ep)
    start_exchange(send_ref, recv_ref, *sems)
    finish_exchange(send_ref, recv_ref, *sems)


def last_kernel(back_ref, slots_of_row_ref, slot_col_ref, grad_ref, u_ref, x_ref, s1_ref, s3_ref, s2_ref, wd_ref, grad_x_ref, pack_ref, mixed_ref, shared_ref):
    back_to_tokens(back_ref, slots_of_row_ref, slot_col_ref, grad_ref, u_ref, x_ref, s1_ref, s3_ref, s2_ref, wd_ref, pack_ref, mixed_ref, shared_ref, grad_x_ref)


def remote(src, dst, send_sem, recv_sem, to):
    return pltpu.make_async_remote_copy(src_ref=src, dst_ref=dst, send_sem=send_sem, recv_sem=recv_sem, device_id=to, device_id_type=MESH)


TILE = 8


def sum_kernel(pack_ref, gate_ref, up_ref, down_ref, dense_out, gate_out, up_out, down_out, pair_ref, total_ref, parts_ref, mine_ref, full_ref, gate_in, up_in, down_in, pair_ssem, pair_rsem, rs_ssem, rs_rsem, ag_ssem, ag_rsem, local_sem):
    me = lax.axis_index("ep")
    core = lax.axis_index("dp")
    other = 1 - core
    ep = parts_ref.shape[0]
    owners = pack_ref.shape[1] // TILE
    barrier = pltpu.get_barrier_semaphore()
    signal_peers(ep)
    pl.semaphore_signal(barrier, inc=1, device_id={"dp": other}, device_id_type=MESH)
    pl.semaphore_wait(barrier, ep)
    partner = {"dp": other}
    pair = [
        remote(pack_ref.at[other], pair_ref, pair_ssem.at[0], pair_rsem.at[0], partner),
        remote(gate_ref, gate_in, pair_ssem.at[1], pair_rsem.at[1], partner),
        remote(up_ref, up_in, pair_ssem.at[2], pair_rsem.at[2], partner),
        remote(down_ref, down_in, pair_ssem.at[3], pair_rsem.at[3], partner),
    ]
    for copy in pair:
        copy.start()
    pair[0].wait_recv()
    summed = (pack_ref[core].astype(F32) + pair_ref[...].astype(F32)).astype(BF16)
    total_ref[...] = summed.reshape(total_ref.shape)

    def scatter(i, carry):
        peer = lax.rem(me + i, ep)

        @pl.when(peer < owners)
        def _():
            remote(total_ref.at[peer], parts_ref.at[me], rs_ssem.at[peer], rs_rsem.at[me], {"ep": peer}).start()

        return carry

    lax.fori_loop(1, ep, scatter, 0)

    def scatter_done(i, carry):
        peer = lax.rem(me + i, ep)

        @pl.when(peer < owners)
        def _():
            remote(total_ref.at[peer], parts_ref.at[me], rs_ssem.at[peer], rs_rsem.at[me], {"ep": peer}).wait_send()

        return carry

    @pl.when(me < owners)
    def _():
        parts_ref[me] = total_ref[me]

        def arrived(i, carry):
            peer = lax.rem(me + i, ep)
            remote(total_ref.at[0], parts_ref.at[peer], rs_ssem.at[peer], rs_rsem.at[peer], {"ep": peer}).wait_recv()
            return carry

        lax.fori_loop(1, ep, arrived, 0)
        mine_ref[...] = jnp.sum(parts_ref[...].astype(F32), axis=0).astype(BF16)

        def gather(i, carry):
            peer = lax.rem(me + i, ep)
            remote(mine_ref, full_ref.at[core, me], ag_ssem.at[peer], ag_rsem.at[me], {"ep": peer}).start()
            return carry

        lax.fori_loop(1, ep, gather, 0)
        full_ref[core, me] = mine_ref[...]

    lax.fori_loop(1, ep, scatter_done, 0)
    for copy, have, came, out in ((pair[1], gate_ref, gate_in, gate_out), (pair[2], up_ref, up_in, up_out), (pair[3], down_ref, down_in, down_out)):
        copy.wait_recv()
        out[...] = (have[...].astype(F32) + came[...].astype(F32)).astype(BF16)

    def gathered(i, carry):
        peer = lax.rem(me + i, ep)

        @pl.when(peer < owners)
        def _():
            remote(mine_ref, full_ref.at[core, peer], ag_ssem.at[peer], ag_rsem.at[peer], {"ep": peer}).wait_recv()

        return carry

    lax.fori_loop(1, ep, gathered, 0)
    swap = remote(full_ref.at[core], full_ref.at[core], pair_ssem.at[4], pair_rsem.at[4], partner)
    swap.start()

    @pl.when(me < owners)
    def _():
        def sent(i, carry):
            peer = lax.rem(me + i, ep)
            remote(mine_ref, full_ref.at[core, me], ag_ssem.at[peer], ag_rsem.at[me], {"ep": peer}).wait_send()
            return carry

        lax.fori_loop(1, ep, sent, 0)

    for copy in pair:
        copy.wait_send()
    swap.wait_send()
    remote(full_ref.at[other], full_ref.at[other], pair_ssem.at[4], pair_rsem.at[4], partner).wait_recv()
    dense_out[...] = full_ref[...].reshape(dense_out.shape)


def solution(mesh):
    ep = mesh.shape["ep"]
    tok_spec = P(ALL_AXES, None)
    route_spec = P(None, ALL_AXES, None)
    exp_spec = P(None, "ep", None, None)
    repl_spec = P(None, None, None)

    def body(act_in, grad_out, slot_ids, gate_vals, w_dense, w_gate, w_up, w_down, ws_gate, ws_up, ws_down):
        tokens, width = act_in.shape
        ff = w_gate.shape[3]
        local = w_gate.shape[1]
        cap = 2 * tokens * 2 // (local * ep)
        wide, half = pad_lanes(width), pad_lanes(ff)
        full = local * width
        block = (ep, cap, full)
        slot_rows = jnp.swapaxes(slot_ids, 1, 2)
        row = np.arange(ep * cap)
        slots_of_row = jnp.asarray(((row // cap) * local * cap + row % cap).astype(np.int32))[None, :]
        send = pltpu.VMEM(block, BF16)
        token_pads = [pltpu.VMEM((tokens, wide), BF16)] * 2
        copy_pads = [pltpu.VMEM((2 * tokens, wide), BF16)] * 2
        weights = [pltpu.VMEM((2, wide, 2 * half), BF16), pltpu.VMEM((2, half, wide), BF16)]
        accs = [pltpu.VMEM((2, wide, 2 * half), F32), pltpu.VMEM((2, half, wide), F32)]
        token_tmp = [pltpu.VMEM((tokens, width), BF16), pltpu.VMEM((tokens, width), F32)]
        sems = exchange_scratch(ep)
        tok = shape((tokens, width))
        pack_lanes = wide + 3 * half
        packed = shape((width, pack_lanes))
        eg = [shape((local, width, ff)), shape((local, width, ff)), shape((local, ff, width))]

        u1, rows1 = call(dispatch_kernel, (act_in, w_dense[0], slot_rows[0]), (tok, shape(block)), [send, *token_pads, *sems], 1)
        (grads2,) = call(grad_dispatch_kernel, (grad_out, gate_vals[1], slot_rows[1]), (shape(block),), [send, *copy_pads, *sems], 2)
        (back1,) = call(forward_kernel, (rows1, w_gate[0], w_up[0], w_down[0]), (shape(block),), [send, *weights, *sems], 3)
        x2, u2, rows2 = call(
            between_kernel,
            (back1, slots_of_row, slot_ids[0], gate_vals[0], u1, ws_gate[0], ws_up[0], ws_down[0], w_dense[1], slot_rows[1]),
            (tok, tok, shape(block)),
            [send, *token_pads, *sems],
            4,
        )
        back2, *eg2 = call(backward_kernel, (rows2, grads2, w_gate[1], w_up[1], w_down[1]), (shape(block), *eg), [send, *weights, *accs, *sems], 5)
        grad_x2, pack2, grads1 = call(
            turn_kernel,
            (back2, slots_of_row, slot_ids[1], grad_out, u2, x2, ws_gate[1], ws_up[1], ws_down[1], w_dense[1], gate_vals[0], slot_rows[0]),
            (tok, packed, shape(block)),
            [send, *copy_pads, *token_tmp, *sems],
            6,
        )
        back3, *eg1 = call(backward_kernel, (rows1, grads1, w_gate[0], w_up[0], w_down[0]), (shape(block), *eg), [send, *weights, *accs, *sems], 5)
        grad_act, pack1 = call(
            last_kernel,
            (back3, slots_of_row, slot_ids[0], grad_x2, u1, act_in, ws_gate[0], ws_up[0], ws_down[0], w_dense[0]),
            (tok, packed),
            token_tmp,
        )
        packs = jnp.stack([pack1, pack2])
        stacked = [jnp.stack([a, b]) for a, b in zip(eg1, eg2)]
        tiles = width // TILE
        es = [s.shape for s in stacked]
        sums, e_gate, e_up, e_down = call(
            sum_kernel,
            (packs, *stacked),
            (shape(packs.shape), *[shape(s) for s in es]),
            [
                pltpu.VMEM((width, pack_lanes), BF16),
                pltpu.VMEM((tiles, TILE, pack_lanes), BF16),
                pltpu.VMEM((ep, TILE, pack_lanes), BF16),
                pltpu.VMEM((TILE, pack_lanes), BF16),
                pltpu.VMEM((2, tiles, TILE, pack_lanes), BF16),
                *[pltpu.VMEM(s, BF16) for s in es],
                pltpu.SemaphoreType.DMA((5,)),
                pltpu.SemaphoreType.DMA((5,)),
                pltpu.SemaphoreType.DMA((ep,)),
                pltpu.SemaphoreType.DMA((ep,)),
                pltpu.SemaphoreType.DMA((ep,)),
                pltpu.SemaphoreType.DMA((ep,)),
                pltpu.SemaphoreType.DMA,
            ],
            7,
        )
        g_dense = sums[:, :, :width]
        g_s1 = sums[:, :, wide : wide + ff]
        g_s3 = sums[:, :, wide + half : wide + half + ff]
        g_s2 = jnp.swapaxes(sums[:, :, wide + 2 * half : wide + 2 * half + ff], 1, 2)
        return (grad_act, g_dense, e_gate, e_up, e_down, g_s1, g_s3, g_s2)

    return jax.shard_map(body, mesh=mesh, in_specs=(tok_spec, tok_spec, route_spec, route_spec, repl_spec, exp_spec, exp_spec, exp_spec, repl_spec, repl_spec, repl_spec), out_specs=(tok_spec, repl_spec, exp_spec, exp_spec, exp_spec, repl_spec, repl_spec, repl_spec), check_vma=False)
```

time: 719 us -> 520 us (0.72)
  Pallas kernels: 0 us -> 467 us
  waiting for transfers between devices: 339 us -> 0 us
  local copies, waits for them, and re-layouts: 159 us -> 32.6 us
  matrix products: 78 us -> 0 us
  starting transfers between devices: 69.1 us -> 0 us
  other arithmetic: 51.2 us -> 8.88 us
  between operations: 15.3 us -> 1.06 us
    pallas_call x0 -> x9, Pallas kernels: none -> 467 us  [call(): pl.pallas_call(kernel, out_shape=outs, in_specs=[vmem() for _ in ins], ou...]
    all_to_all x7 -> x0, waiting for transfers between devices: 192 us -> none  [the longest x2 85.5 us: layer_front(): lax.all_to_all(send_buf, 'ep', 0, 1)]
    psum x2 -> x0, waiting for transfers between devices: 147 us -> none  [the longest x1 147 us: body(): dense_sums[layer] = [lax.psum(part, ALL_AXES) for part in dense_grads]]
    dot_general x40 -> x0, matrix products: 78 us -> none  [the longest x8 14 us: contract_rows(): lax.dot_general(left, right, (((0,), (0,)), ((), ())), preferred_element_...]
    gather x7 -> x0, local copies, waits for them, and re-layouts: 71.2 us -> none  [the longest x2 26.6 us: layer_front(): jnp.take(mixed_ext, tok_owner, axis=0)]
    all_to_all x7 -> x0, starting transfers between devices: 68.8 us -> none  [the longest x2 22.3 us: layer_front(): lax.all_to_all(send_buf, 'ep', 0, 1)]
    convert_element_type x8 -> x0, local copies, waits for them, and re-layouts: 20.5 us -> none  [the longest x2 6.72 us: layer_backward(): jnp.take(grad_back, slot_flat, axis=0).reshape(tokens, top, width)]
    reduce_sum x3 -> x0, other arithmetic: 18.2 us -> none  [the longest x2 11.4 us: layer_backward(): jnp.sum(jnp.take(grad_back, slot_flat, axis=0).reshape(tokens, top, width...]
  transfers between devices with their start and end apart: 9 -> 0, of which waited for: 7 -> 0; matrix products, arithmetic and copies ran while one was open for 21% -> 0% of each run, Pallas kernels for 0% -> 0%
where the time goes in v1:
time: 520 us; the launch traced here: 510 us
  Pallas kernels  467 us (90%)
  local copies, waits for them, and re-layouts  32.6 us (6%)
  other arithmetic  8.88 us (2%)
    pallas_call x9, Pallas kernels, call(): pl.pallas_call(kernel, out_shape=outs, in_specs=[vmem() for _ in ins], ou...  467 us
    unnamed x59, local copies, waits for them, and re-layouts  23.5 us

profile of v1, /device:TPU:1, one launch (start us, length us, event | category | flops | bytes accessed | tf_op | source)
XLA Modules:
  0.0 509.8 jit_solution(15758304262899269801)
XLA Ops:
  0.7 2.2 slice_bitcast_fusion.3
  3.5 1.2 copy.20.x_ref
  4.6 52.0 %shard_map.179 = (bf16[768,448]{1,0:T(8,128)(2,1)}, bf16[64,24,896]{2,1,0:T(8,128)(2,1)}) custom-call(bf16[768,448]{1,0:T(8,128)(2,1)} %copy.20.x_ref, bf16[448,448]{1,0:T(8,128)(2,1)} %get-tuple-element.70.wd_ref, s32[2,768]{1,0:T(2,128)} %get-tuple-element.82.slot_row_ref), custom_call_target="tpu_custom_call" | custom-call | tf_op jit(solution)/shard_map/pallas_call | solution.py:262
  56.7 1.1 copy.42
  58.3 1.1 copy.43
  59.8 1.1 slice_bitcast_fusion.1
  60.9 50.8 %shard_map.180.back_ref = bf16[64,24,896]{2,1,0:T(8,128)(2,1)} custom-call(bf16[64,24,896]{2,1,0:T(8,128)(2,1)} %get-tuple-element.30.rows_ref, bf16[2,448,304]{2,1,0:T(8,128)(2,1)} %bitcast.39, bf16[2,448,304]{2,1,0:T(8,128)(2,1)} %bitcast.41, bf16[2,304,448]{2,1,0:T(8,128)(2,1)} %get-tuple-element.64.down_ref), custom_call_target="tpu_custom_call" | custom-call | tf_op jit(solution)/shard_map/pallas_call | solution.py:262
  114.7 0.9 copy.44
  115.6 1.0 copy.45
  116.6 51.5 %shard_map.181 = (bf16[768,448]{1,0:T(8,128)(2,1)}, bf16[768,448]{1,0:T(8,128)(2,1)}, bf16[64,24,896]{2,1,0:T(8,128)(2,1)}) custom-call(bf16[64,24,896]{2,1,0:T(8,128)(2,1)} %shard_map.180.back_ref, s32[1,1536]{1,0:T(1,128)} %constant.6.slots_of_row_ref, s32[768,2]{1,0:T(8,128)} %bitcast.43, f32[768,2]{1,0:T(8,128)} %bitcast.45, ...), custom_call_target="tpu_custom_call" | custom-call | tf_op jit(solution)/shard_map/pallas_call | solution.py:262
  168.0 1.2 copy.28.grad_ref
  169.2 0.9 copy.48
  170.1 50.6 %shard_map.182.grads_ref = bf16[64,24,896]{2,1,0:T(8,128)(2,1)} custom-call(bf16[768,448]{1,0:T(8,128)(2,1)} %copy.28.grad_ref, f32[768,2]{1,0:T(8,128)} %bitcast.53, s32[2,768]{1,0:T(2,128)} %get-tuple-element.81.slot_row_ref), custom_call_target="tpu_custom_call" | custom-call | tf_op jit(solution)/shard_map/pallas_call | solution.py:262
  220.7 1.1 copy.49
  221.9 1.1 copy.50
  223.0 55.4 %shard_map.183 = (bf16[64,24,896]{2,1,0:T(8,128)(2,1)}, bf16[2,448,304]{2,1,0:T(8,128)(2,1)}, bf16[2,448,304]{2,1,0:T(8,128)(2,1)}, bf16[2,304,448]{2,1,0:T(8,128)(2,1)}) custom-call(bf16[64,24,896]{2,1,0:T(8,128)(2,1)} %get-tuple-element.32.rows_ref, bf16[64,24,896]{2,1,0:T(8,128)(2,1)} %shard_map.182.grads_ref, bf16[2,448,304]{2,1,0:T(8,128)(2,1)} %bitcast.51, ...), custom_call_target="tpu_custom_call" | custom-call | tf_op jit(solution)/shard_map/pallas_call | solution.py:262
  281.2 65.3 %shard_map.184 = (bf16[768,448]{1,0:T(8,128)(2,1)}, bf16[448,1664]{1,0:T(8,128)(2,1)}, bf16[64,24,896]{2,1,0:T(8,128)(2,1)}) custom-call(bf16[64,24,896]{2,1,0:T(8,128)(2,1)} %get-tuple-element.33.back_ref, s32[1,1536]{1,0:T(1,128)} %constant.6.slots_of_row_ref, s32[768,2]{1,0:T(8,128)} %bitcast.54, bf16[768,448]{1,0:T(8,128)(2,1)} %copy.28.grad_ref, ...), custom_call_target="tpu_custom_call" | custom-call | tf_op jit(solution)/shard_map/pallas_call | solution.py:262
  346.5 58.0 %shard_map.185 = (bf16[64,24,896]{2,1,0:T(8,128)(2,1)}, bf16[2,448,304]{2,1,0:T(8,128)(2,1)}, bf16[2,448,304]{2,1,0:T(8,128)(2,1)}, bf16[2,304,448]{2,1,0:T(8,128)(2,1)}) custom-call(bf16[64,24,896]{2,1,0:T(8,128)(2,1)} %get-tuple-element.30.rows_ref, bf16[64,24,896]{2,1,0:T(8,128)(2,1)} %get-tuple-element.36.grads_ref, bf16[2,448,304]{2,1,0:T(8,128)(2,1)} %bitcast.40, ...), custom_call_target="tpu_custom_call" | custom-call | tf_op jit(solution)/shard_map/pallas_call | solution.py:262
  404.5 2.4 pad_maximum_fusion.3.down_ref
  406.9 3.2 pad_maximum_fusion.1
  410.2 11.3 %shard_map.186 = (bf16[768,448]{1,0:T(8,128)(2,1)}, bf16[448,1664]{1,0:T(8,128)(2,1)}) custom-call(bf16[64,24,896]{2,1,0:T(8,128)(2,1)} %get-tuple-element.37.back_ref, s32[1,1536]{1,0:T(1,128)} %constant.6.slots_of_row_ref, s32[768,2]{1,0:T(8,128)} %bitcast.44, bf16[768,448]{1,0:T(8,128)(2,1)} %get-tuple-element.38.grad_ref, ...), custom_call_target="tpu_custom_call" | custom-call | tf_op jit(solution)/shard_map/pallas_call | solution.py:262
  421.4 3.3 pad_maximum_fusion.pack_ref
  424.7 72.4 %shard_map.187 = (bf16[2,448,1664]{2,1,0:T(8,128)(2,1)}, bf16[2,2,448,304]{3,2,1,0:T(8,128)(2,1)}, bf16[2,2,448,304]{3,2,1,0:T(8,128)(2,1)}, bf16[2,2,304,448]{3,2,1,0:T(8,128)(2,1)}) custom-call(bf16[2,448,1664]{2,1,0:T(8,128)(2,1)} %pad_maximum_fusion.pack_ref, bf16[2,2,448,304]{3,2,1,0:T(8,128)(2,1)} %get-tuple-element.83.gate_ref, ...), custom_call_target="tpu_custom_call" | custom-call | tf_op jit(solution)/shard_map/pallas_call | solution.py:262
  497.1 1.7 slice_bitcast_fusion
  498.9 1.1 copy.39
  500.0 1.1 copy.40
  501.1 1.1 copy.41
  502.1 1.5 copy.37
  503.7 1.5 copy.38
  505.2 2.3 slice.104
  507.5 1.1 copy.36
  508.6 1.0 copy.55
  (51 shorter events, 7.2 us)
Async XLA Ops:
  0.6 2.2 copy-start.17
  0.6 2.8 copy-start.8
  2.9 53.8 %copy-start.3 = (bf16[2,2,448,304]{2,3,1,0:T(8,128)(2,1)S(1)}, bf16[2,2,448,304]{2,3,1,0:T(8,128)(2,1)}, u32[]{:S(2)}) copy-start(bf16[2,2,448,304]{2,3,1,0:T(8,128)(2,1)} %param.17) | copy-start | bytes 3268612
  56.7 1.5 copy-start.4
  58.3 1.5 copy-start.5
  60.9 50.8 %copy-start.13 = (bf16[2,448,304]{1,2,0:T(8,128)(2,1)S(1)}, bf16[2,448,304]{1,2,0:T(8,128)(2,1)}, u32[]{:S(2)}) copy-start(bf16[2,448,304]{1,2,0:T(8,128)(2,1)} %param.20) | copy-start | bytes 1634308
  111.7 1.1 copy-start.14
  111.8 2.0 copy-start.15
  112.9 2.7 copy-start.18
  116.6 51.5 %copy-start.9 = (bf16[768,448]{0,1:T(8,128)(2,1)S(1)}, bf16[768,448]{0,1:T(8,128)(2,1)}, u32[]{:S(2)}) copy-start(bf16[768,448]{0,1:T(8,128)(2,1)} %param.13) | copy-start | bytes 2064388
  346.5 58.0 %copy-start.16 = (bf16[2,304,448]{2,1,0:T(8,128)(2,1)S(1)}, bf16[2,304,448]{2,1,0:T(8,128)(2,1)}, u32[]{:S(2)}) copy-start(bf16[2,304,448]{2,1,0:T(8,128)(2,1)} %get-tuple-element.47) | copy-start | bytes 1634308
  404.5 2.4 copy-start.10
  404.5 2.4 copy-start.11
  404.5 2.4 copy-start.12
  410.2 11.3 %copy-start = (bf16[448,1664]{1,0:T(8,128)(2,1)S(1)}, bf16[448,1664]{1,0:T(8,128)(2,1)}, u32[]{:S(2)}) copy-start(bf16[448,1664]{1,0:T(8,128)(2,1)} %get-tuple-element.41) | copy-start | bytes 4472836
  500.0 2.2 copy-start.2
  502.1 1.5 copy-start.1
  505.2 2.3 copy-start.7
  505.2 3.4 copy-start.6

commit v2 on v1

v2 whole, which is shorter than its diff:
```python
import functools
import jax
import jax.numpy as jnp
import numpy as np
from jax import lax
from jax.experimental import pallas as pl
from jax.experimental.pallas import tpu as pltpu
from jax.sharding import PartitionSpec as P

ALL_AXES = ("ep", "dp")
MESH = pl.DeviceIdType.MESH
LANE = 128
VMEM_LIMIT = 60 * 1024 * 1024
F32 = jnp.float32
BF16 = jnp.bfloat16


def pad_lanes(n):
    return (n + LANE - 1) // LANE * LANE


def dot(a, b):
    return lax.dot_general(a, b, (((1,), (0,)), ((), ())), preferred_element_type=F32)


def dot_rows(a, b):
    return lax.dot_general(a, b, (((0,), (0,)), ((), ())), preferred_element_type=F32)


def dot_cols(a, b):
    return lax.dot_general(a, b, (((1,), (1,)), ((), ())), preferred_element_type=F32)


def onehot(cond):
    return jnp.where(cond, 1.0, 0.0).astype(BF16)


def silu(x):
    return x * jax.nn.sigmoid(x)


def silu_grad(x):
    sigma = jax.nn.sigmoid(x)
    return sigma * (1.0 + x * (1.0 - sigma))


def roll_up(x, by):
    return pltpu.roll(x.astype(F32), by, 1)


def join(first, second):
    wide = first.shape[1]
    return jnp.concatenate([first[:, : wide - LANE], first[:, wide - LANE :] + second[:, :LANE], second[:, LANE:]], axis=1)


def spread(lo_ref, hi_ref, rows, at):
    width = rows.shape[1]
    wide = lo_ref.shape[1]
    count = rows.shape[0]
    lo_ref[at : at + count, :] = jnp.zeros((count, wide), BF16)
    lo_ref[at : at + count, :width] = rows
    hi_ref[at : at + count, :] = roll_up(lo_ref[at : at + count, :], wide - width).astype(BF16)


CHUNK = 8
GROUP = 32


def fill_send(slot_rows, lo_ref, hi_ref, send_ref, chunk, per_copy):
    ep, cap, _ = send_ref.shape
    tokens = slot_rows.shape[1]
    row0 = slot_rows[0:1, :]
    row1 = slot_rows[1:2, :]
    rows = pl.ds(chunk * CHUNK, CHUNK)

    def body(step, carry):
        dims = (GROUP, CHUNK, tokens)
        slot = (lax.broadcasted_iota(jnp.int32, dims, 0) + step * GROUP) * (2 * cap) + lax.broadcasted_iota(jnp.int32, dims, 1)
        slot = slot.reshape(GROUP * CHUNK, tokens) + chunk * CHUNK

        def pick(s):
            if per_copy:
                return jnp.concatenate([onehot(row0 == s), onehot(row1 == s)], axis=1)
            return onehot((row0 == s) | (row1 == s))

        first = dot(pick(slot), lo_ref[...])
        second = dot(pick(slot + cap), hi_ref[...])
        send_ref[pl.ds(step * GROUP, GROUP), rows] = join(first, second).astype(BF16).reshape(GROUP, CHUNK, send_ref.shape[2])
        return carry

    lax.fori_loop(0, ep // GROUP, body, 0)


def halves(ref, width, step=None, chunk=None):
    full = ref.shape[2]
    wide = pad_lanes(width)
    block = ref[...] if step is None else ref[pl.ds(step * GROUP, GROUP), pl.ds(chunk * CHUNK, CHUNK)]
    block = block.reshape(block.shape[0] * block.shape[1], full)
    return block[:, :wide], block[:, full - wide :]


def collect(back_ref, slot_cols, slots_of_row, gate_cols, width, start, count):
    cap = back_ref.shape[1]
    first, second = halves(back_ref, width)
    cols = slot_cols[start : start + count, :]
    col0 = cols[:, 0:1]
    col1 = cols[:, 1:2]
    if gate_cols is None:
        acc0 = dot(onehot((col0 == slots_of_row) | (col1 == slots_of_row)), first)
        acc1 = dot(onehot((col0 == slots_of_row + cap) | (col1 == slots_of_row + cap)), second)
    else:
        gates = gate_cols[start : start + count, :]
        acc0 = gates[:, 0:1] * dot(onehot(col0 == slots_of_row), first) + gates[:, 1:2] * dot(onehot(col1 == slots_of_row), first)
        acc1 = gates[:, 0:1] * dot(onehot(col0 == slots_of_row + cap), second) + gates[:, 1:2] * dot(onehot(col1 == slots_of_row + cap), second)
    return (acc0 + roll_up(acc1, width))[:, :width]


def load_experts(gate_ref, up_ref, down_ref, w13_ref, w2_ref):
    width, ff = gate_ref.shape[1], gate_ref.shape[2]
    wide = w13_ref.shape[1]
    half = w13_ref.shape[2] // 2
    w13_ref[...] = jnp.zeros(w13_ref.shape, BF16)
    w2_ref[...] = jnp.zeros(w2_ref.shape, BF16)
    for e in range(2):
        at = e * (wide - width)
        w13_ref[e, at : at + width, :ff] = gate_ref[e]
        w13_ref[e, at : at + width, half : half + ff] = up_ref[e]
        w2_ref[e, :ff, :width] = down_ref[e]
    w2_ref[1] = roll_up(w2_ref[1], wide - width).astype(BF16)


def experts_forward(recv_ref, w13_ref, w2_ref, send_ref, width, chunk):
    ep, cap, full = recv_ref.shape
    half = w13_ref.shape[2] // 2

    def body(step, carry):
        rows = halves(recv_ref, width, step, chunk)
        outs = []
        for e in range(2):
            pre = dot(rows[e], w13_ref[e])
            hidden = (silu(pre[:, :half]) * pre[:, half:]).astype(BF16)
            outs.append(dot(hidden, w2_ref[e]))
        send_ref[pl.ds(step * GROUP, GROUP), pl.ds(chunk * CHUNK, CHUNK)] = join(outs[0], outs[1]).astype(BF16).reshape(GROUP, CHUNK, full)
        return carry

    lax.fori_loop(0, ep // GROUP, body, 0)


def experts_backward(recv_ref, grad_ref, w13_ref, w2_ref, send_ref, acc13_ref, acc2_ref, width, chunk):
    ep, cap, full = recv_ref.shape
    half = w13_ref.shape[2] // 2
    if chunk == 0:
        acc13_ref[...] = jnp.zeros(acc13_ref.shape, F32)
        acc2_ref[...] = jnp.zeros(acc2_ref.shape, F32)

    def body(step, carry):
        rows = halves(recv_ref, width, step, chunk)
        grads = halves(grad_ref, width, step, chunk)
        outs = []
        for e in range(2):
            pre = dot(rows[e], w13_ref[e])
            one, three = pre[:, :half], pre[:, half:]
            act = silu(one)
            hidden = (act * three).astype(BF16)
            grad_hidden = dot_cols(grads[e], w2_ref[e])
            grad_one = (grad_hidden * three * silu_grad(one)).astype(BF16)
            grad_three = (grad_hidden * act).astype(BF16)
            grad_pre = jnp.concatenate([grad_one, grad_three], axis=1)
            outs.append(dot_cols(grad_pre, w13_ref[e]))
            acc13_ref[e] += dot_rows(rows[e], grad_pre)
            acc2_ref[e] += dot_rows(hidden, grads[e])
        send_ref[pl.ds(step * GROUP, GROUP), pl.ds(chunk * CHUNK, CHUNK)] = join(outs[0], outs[1]).astype(BF16).reshape(GROUP, CHUNK, full)
        return carry

    lax.fori_loop(0, ep // GROUP, body, 0)


def store_expert_grads(acc13_ref, acc2_ref, gate_out, up_out, down_out):
    width, ff = gate_out.shape[1], gate_out.shape[2]
    wide = acc13_ref.shape[1]
    half = acc13_ref.shape[2] // 2
    for e in range(2):
        at = e * (wide - width)
        gate_out[e] = acc13_ref[e, at : at + width, :ff].astype(BF16)
        up_out[e] = acc13_ref[e, at : at + width, half : half + ff].astype(BF16)
        down = acc2_ref[e]
        if e:
            down = roll_up(down, width)
        down_out[e] = down[:ff, :width].astype(BF16)


def dense_front(x, w_dense_ref):
    return (x.astype(F32) + dot(x, w_dense_ref[...])).astype(BF16)


def signal_peers(ep):
    barrier = pltpu.get_barrier_semaphore()
    me = lax.axis_index("ep")

    def body(i, carry):
        pl.semaphore_signal(barrier, inc=1, device_id={"ep": lax.rem(me + i, ep)}, device_id_type=MESH)
        return carry

    lax.fori_loop(1, ep, body, 0)


def wait_peers(ep):
    pl.semaphore_wait(pltpu.get_barrier_semaphore(), ep - 1)


def peer_of(i, ep):
    me = lax.axis_index("ep")
    turn = lax.rem(i - 1 + (ep // 2) * lax.axis_index("dp"), ep - 1) + 1
    return lax.rem(me + turn, ep)


def remote(src, dst, send_sem, recv_sem, to):
    return pltpu.make_async_remote_copy(src_ref=src, dst_ref=dst, send_sem=send_sem, recv_sem=recv_sem, device_id=to, device_id_type=MESH)


class Exchange:
    def __init__(self, send, recv, send_sem, recv_sem, local_sem):
        self.send, self.recv, self.send_sem, self.recv_sem, self.local_sem = send, recv, send_sem, recv_sem, local_sem
        self.ep, cap, _ = send.shape
        self.chunks = cap // CHUNK
        self.me = lax.axis_index("ep")

    def copy(self, chunk, peer, to):
        rows = pl.ds(chunk * CHUNK, CHUNK)
        return remote(self.send.at[peer, rows], self.recv.at[to, rows], self.send_sem.at[chunk, peer], self.recv_sem.at[chunk, to], {"ep": peer})

    def own(self, chunk):
        rows = pl.ds(chunk * CHUNK, CHUNK)
        return pltpu.make_async_copy(self.send.at[self.me, rows], self.recv.at[self.me, rows], self.local_sem.at[chunk])

    def start(self, chunk):
        def body(i, carry):
            self.copy(chunk, peer_of(i, self.ep), self.me).start()
            return carry

        lax.fori_loop(1, self.ep, body, 0)
        self.own(chunk).start()

    def wait_recv(self, chunk):
        self.own(chunk).wait()

        def body(i, carry):
            peer = lax.rem(self.me + i, self.ep)
            self.copy(chunk, peer, peer).wait_recv()
            return carry

        lax.fori_loop(1, self.ep, body, 0)

    def wait_send(self):
        for chunk in range(self.chunks):

            def body(i, carry):
                self.copy(chunk, lax.rem(self.me + i, self.ep), self.me).wait_send()
                return carry

            lax.fori_loop(1, self.ep, body, 0)


def vmem():
    return pl.BlockSpec(memory_space=pltpu.VMEM)


def call(kernel, ins, outs, scratch, collective_id=None):
    return pl.pallas_call(
        kernel,
        out_shape=outs,
        in_specs=[vmem() for _ in ins],
        out_specs=tuple(vmem() for _ in outs),
        scratch_shapes=scratch,
        compiler_params=pltpu.CompilerParams(collective_id=collective_id, has_side_effects=collective_id is not None, vmem_limit_bytes=VMEM_LIMIT),
    )(*ins)


def exchange_scratch(ep, cap):
    return [pltpu.SemaphoreType.DMA((cap // CHUNK, ep)), pltpu.SemaphoreType.DMA((cap // CHUNK, ep)), pltpu.SemaphoreType.DMA((cap // CHUNK,))]


def shape(dims, dtype=BF16):
    return jax.ShapeDtypeStruct(dims, dtype)


def shared_out(u, s1_ref, s3_ref, s2_ref):
    one = dot(u, s1_ref[...])
    three = dot(u, s3_ref[...])
    return dot((silu(one) * three).astype(BF16), s2_ref[...])


def spread_gated(grad, gate_col_ref, lo_ref, hi_ref, start):
    tokens = gate_col_ref.shape[0]
    count = grad.shape[0]
    gates = gate_col_ref[start : start + count, :]
    for j in range(2):
        spread(lo_ref, hi_ref, (gates[:, j : j + 1] * grad.astype(F32)).astype(BF16), j * tokens + start)


def first_kernel(x_ref, wd_ref, slot_row_ref, gate_ref, up_ref, down_ref, grad_ref, gate_col_ref, grad_slot_row_ref, u_ref, rows_ref, grads_ref, back_ref, send_ref, lo_ref, hi_ref, grad_send_ref, grad_lo_ref, grad_hi_ref, back_send_ref, w13_ref, w2_ref, *sems):
    ep = rows_ref.shape[0]
    width = x_ref.shape[1]
    signal_peers(ep)
    out = Exchange(send_ref, rows_ref, *sems[0:3])
    grads = Exchange(grad_send_ref, grads_ref, *sems[3:6])
    back = Exchange(back_send_ref, back_ref, *sems[6:9])
    u = dense_front(x_ref[...], wd_ref)
    u_ref[...] = u
    spread(lo_ref, hi_ref, u, 0)
    for chunk in range(out.chunks):
        fill_send(slot_row_ref[...], lo_ref, hi_ref, send_ref, chunk, False)
        if chunk == 0:
            wait_peers(ep)
        out.start(chunk)
    load_experts(gate_ref, up_ref, down_ref, w13_ref, w2_ref)
    spread_gated(grad_ref[...], gate_col_ref, grad_lo_ref, grad_hi_ref, 0)
    for chunk in range(out.chunks):
        fill_send(grad_slot_row_ref[...], grad_lo_ref, grad_hi_ref, grad_send_ref, chunk, True)
    for chunk in range(out.chunks):
        out.wait_recv(chunk)
        experts_forward(rows_ref, w13_ref, w2_ref, back_send_ref, width, chunk)
        back.start(chunk)
        grads.start(chunk)
    for chunk in range(out.chunks):
        grads.wait_recv(chunk)
        back.wait_recv(chunk)
    for e in (out, grads, back):
        e.wait_send()


def middle_kernel(back_ref, slots_of_row_ref, slot_col_ref, gate_col_ref, u1_ref, s1_ref, s3_ref, s2_ref, wd_ref, slot_row_ref, grads_ref, gate_ref, up_ref, down_ref, x_ref, u_ref, ret_ref, g_gate_ref, g_up_ref, g_down_ref, rows_ref, send_ref, lo_ref, hi_ref, ret_send_ref, w13_ref, w2_ref, acc13_ref, acc2_ref, *sems):
    ep = rows_ref.shape[0]
    tokens, width = u1_ref.shape
    signal_peers(ep)
    out = Exchange(send_ref, rows_ref, *sems[0:3])
    ret = Exchange(ret_send_ref, ret_ref, *sems[3:6])
    count = 256
    for start in range(0, tokens, count):
        u = u1_ref[start : start + count, :]
        routed = collect(back_ref, slot_col_ref, slots_of_row_ref[...], gate_col_ref, width, start, count)
        x = (u.astype(F32) + routed + shared_out(u, s1_ref, s3_ref, s2_ref)).astype(BF16)
        x_ref[start : start + count, :] = x
        mixed = dense_front(x, wd_ref)
        u_ref[start : start + count, :] = mixed
        spread(lo_ref, hi_ref, mixed, start)
    for chunk in range(out.chunks):
        fill_send(slot_row_ref[...], lo_ref, hi_ref, send_ref, chunk, False)
        if chunk == 0:
            wait_peers(ep)
        out.start(chunk)
    load_experts(gate_ref, up_ref, down_ref, w13_ref, w2_ref)
    for chunk in range(out.chunks):
        out.wait_recv(chunk)
        experts_backward(rows_ref, grads_ref, w13_ref, w2_ref, ret_send_ref, acc13_ref, acc2_ref, width, chunk)
        ret.start(chunk)
    store_expert_grads(acc13_ref, acc2_ref, g_gate_ref, g_up_ref, g_down_ref)
    for chunk in range(out.chunks):
        ret.wait_recv(chunk)
    for e in (out, ret):
        e.wait_send()


def shared_back(grad, u, s1_ref, s3_ref, s2_ref, hid_ref, one_ref, three_ref):
    one = dot(u, s1_ref[...])
    three = dot(u, s3_ref[...])
    act = silu(one)
    hid_ref[...] = (act * three).astype(BF16)
    grad_hidden = dot_cols(grad, s2_ref[...])
    one_ref[...] = (grad_hidden * three * silu_grad(one)).astype(BF16)
    three_ref[...] = (grad_hidden * act).astype(BF16)
    return dot_cols(one_ref[...], s1_ref[...]) + dot_cols(three_ref[...], s3_ref[...])


TILE = 8


class DenseSum:
    def __init__(self, pack, full, pair, total, parts, mine, pair_ssem, pair_rsem, rs_ssem, rs_rsem, ag_ssem, ag_rsem):
        self.pack, self.full, self.pair, self.total, self.parts, self.mine = pack, full, pair, total, parts, mine
        self.pair_ssem, self.pair_rsem = pair_ssem, pair_rsem
        self.rs_ssem, self.rs_rsem, self.ag_ssem, self.ag_rsem = rs_ssem, rs_rsem, ag_ssem, ag_rsem
        self.me = lax.axis_index("ep")
        self.core = lax.axis_index("dp")
        self.ep = parts.shape[0]
        self.owners = total.shape[0]

    def each(self, act, owners=False):
        def body(i, carry):
            peer = lax.rem(self.me + i, self.ep)
            if owners:
                pl.when(peer < self.owners)(lambda: act(peer))
            else:
                act(peer)
            return carry

        lax.fori_loop(1, self.ep, body, 0)

    def pair_copy(self):
        return remote(self.pack.at[1 - self.core], self.pair, self.pair_ssem.at[0], self.pair_rsem.at[0], {"dp": 1 - self.core})

    def scatter_copy(self, peer, tile, to):
        return remote(self.total.at[tile], self.parts.at[to], self.rs_ssem.at[peer], self.rs_rsem.at[to], {"ep": peer})

    def gather_copy(self, peer, to):
        return remote(self.mine, self.full.at[self.core, to], self.ag_ssem.at[peer], self.ag_rsem.at[to], {"ep": peer})

    def swap_copy(self, half):
        return remote(self.full.at[half], self.full.at[half], self.pair_ssem.at[1], self.pair_rsem.at[1], {"dp": 1 - self.core})

    def start_pair(self):
        self.pair_copy().start()

    def scatter(self):
        self.pair_copy().wait_recv()
        both = (self.pack[self.core].astype(F32) + self.pair[...].astype(F32)).astype(BF16)
        self.total[...] = both.reshape(self.total.shape)
        self.each(lambda peer: self.scatter_copy(peer, peer, self.me).start(), owners=True)

    def gather(self):
        @pl.when(self.me < self.owners)
        def _():
            self.parts[self.me] = self.total[self.me]
            self.each(lambda peer: self.scatter_copy(peer, 0, peer).wait_recv())
            self.mine[...] = jnp.sum(self.parts[...].astype(F32), axis=0).astype(BF16)
            self.each(lambda peer: self.gather_copy(peer, self.me).start())
            self.full[self.core, self.me] = self.mine[...]

        self.each(lambda peer: self.scatter_copy(peer, peer, self.me).wait_send(), owners=True)

    def swap(self):
        self.each(lambda peer: self.gather_copy(peer, peer).wait_recv(), owners=True)
        self.swap_copy(self.core).start()

        @pl.when(self.me < self.owners)
        def _():
            self.each(lambda peer: self.gather_copy(peer, self.me).wait_send())

    def finish(self):
        self.pair_copy().wait_send()
        self.swap_copy(self.core).wait_send()
        self.swap_copy(1 - self.core).wait_recv()


def sum_scratch(ep, rows, lanes):
    tiles = rows // TILE
    return [
        pltpu.VMEM((rows, lanes), BF16),
        pltpu.VMEM((tiles, TILE, lanes), BF16),
        pltpu.VMEM((ep, TILE, lanes), BF16),
        pltpu.VMEM((TILE, lanes), BF16),
        pltpu.SemaphoreType.DMA((2,)),
        pltpu.SemaphoreType.DMA((2,)),
        *[pltpu.SemaphoreType.DMA((ep,))] * 4,
    ]


def signal_partner():
    pl.semaphore_signal(pltpu.get_barrier_semaphore(), inc=1, device_id={"dp": 1 - lax.axis_index("dp")}, device_id_type=MESH)


def wait_everyone(ep):
    pl.semaphore_wait(pltpu.get_barrier_semaphore(), ep)


def turn_kernel(ret2_ref, slots_of_row_ref, slot_col_ref, grad_ref, u2_ref, x2_ref, s1_ref, s3_ref, s2_ref, wd_ref, gate_col_ref, slot_row_ref, rows_ref, gate_ref, up_ref, down_ref, u1_ref, s1a_ref, s3a_ref, s2a_ref, grad_x_ref, shared_ref, ret_ref, g_gate_ref, g_up_ref, g_down_ref, full_ref, grads_ref, send_ref, lo_ref, hi_ref, ret_send_ref, w13_ref, w2_ref, acc13_ref, acc2_ref, mixed_ref, hid_ref, one_ref, three_ref, pack_ref, *rest):
    ep = rows_ref.shape[0]
    tokens, width = u2_ref.shape
    ff = s1_ref.shape[1]
    wide, half = pad_lanes(width), pad_lanes(ff)
    signal_peers(ep)
    signal_partner()
    out = Exchange(send_ref, grads_ref, *rest[0:3])
    ret = Exchange(ret_send_ref, ret_ref, *rest[3:6])
    dense = DenseSum(pack_ref, full_ref, *rest[6:16])
    shared_ref[...] = shared_back(grad_ref[...], u2_ref[...], s1_ref, s3_ref, s2_ref, hid_ref, one_ref, three_ref)
    count = 256
    for start in range(0, tokens, count):
        rows = slice(start, start + count)
        routed = collect(ret2_ref, slot_col_ref, slots_of_row_ref[...], None, width, start, count)
        mixed = (grad_ref[rows, :].astype(F32) + routed + shared_ref[rows, :]).astype(BF16)
        mixed_ref[rows, :] = mixed
        grad_x = (mixed.astype(F32) + dot_cols(mixed, wd_ref[...])).astype(BF16)
        grad_x_ref[rows, :] = grad_x
        spread_gated(grad_x, gate_col_ref, lo_ref, hi_ref, start)
    for chunk in range(out.chunks):
        fill_send(slot_row_ref[...], lo_ref, hi_ref, send_ref, chunk, True)
        if chunk == 0:
            wait_everyone(ep)
        out.start(chunk)
    load_experts(gate_ref, up_ref, down_ref, w13_ref, w2_ref)
    pack_ref[...] = jnp.zeros(pack_ref.shape, BF16)
    pack_ref[0, :, :width] = dot_rows(x2_ref[...], mixed_ref[...]).astype(BF16)
    pack_ref[0, :, wide : wide + ff] = dot_rows(u2_ref[...], one_ref[...]).astype(BF16)
    pack_ref[1, :, :ff] = dot_rows(u2_ref[...], three_ref[...]).astype(BF16)
    pack_ref[1, :, half : half + ff] = dot_rows(grad_ref[...], hid_ref[...]).astype(BF16)
    shared_ref[...] = shared_back(grad_x_ref[...], u1_ref[...], s1a_ref, s3a_ref, s2a_ref, hid_ref, one_ref, three_ref)
    pack_ref[0, :, wide + half : wide + half + ff] = dot_rows(u1_ref[...], one_ref[...]).astype(BF16)
    pack_ref[1, :, 2 * half : 2 * half + ff] = dot_rows(u1_ref[...], three_ref[...]).astype(BF16)
    pack_ref[1, :, 3 * half : 3 * half + ff] = dot_rows(grad_x_ref[...], hid_ref[...]).astype(BF16)
    dense.start_pair()
    for chunk in range(out.chunks):
        out.wait_recv(chunk)
        experts_backward(rows_ref, grads_ref, w13_ref, w2_ref, ret_send_ref, acc13_ref, acc2_ref, width, chunk)
        ret.start(chunk)
        if chunk == 0:
            dense.scatter()
    store_expert_grads(acc13_ref, acc2_ref, g_gate_ref, g_up_ref, g_down_ref)
    dense.gather()
    for chunk in range(out.chunks):
        ret.wait_recv(chunk)
    dense.swap()
    for e in (out, ret):
        e.wait_send()
    dense.finish()


def last_kernel(ret_ref, slots_of_row_ref, slot_col_ref, grad_ref, shared_ref, x_ref, wd_ref, sums_ref, gate1_ref, up1_ref, down1_ref, gate2_ref, up2_ref, down2_ref, grad_x_ref, dense_out, gate_out, up_out, down_out, s1_out, s3_out, s2_out, mixed_ref, pack_ref, full_ref, gate_in, up_in, down_in, e_ssem, e_rsem, *sums):
    tokens, width = x_ref.shape
    ff = s1_out.shape[2]
    wide, half = pad_lanes(width), pad_lanes(ff)
    dense = DenseSum(pack_ref, full_ref, *sums)
    signal_peers(dense.ep)
    signal_partner()
    other = {"dp": 1 - dense.core}
    mine = ((gate1_ref, gate2_ref, gate_in, gate_out), (up1_ref, up2_ref, up_in, up_out), (down1_ref, down2_ref, down_in, down_out))
    pairs = [(remote(refs[k], refs[2].at[k], e_ssem.at[n, k], e_rsem.at[n, k], other)) for n, refs in enumerate(mine) for k in range(2)]
    wait_everyone(dense.ep)
    for copy in pairs:
        copy.start()
    count = 256
    for start in range(0, tokens, count):
        rows = slice(start, start + count)
        routed = collect(ret_ref, slot_col_ref, slots_of_row_ref[...], None, width, start, count)
        mixed_ref[rows, :] = (grad_ref[rows, :].astype(F32) + routed + shared_ref[rows, :]).astype(BF16)
    part = dot_rows(x_ref[...], mixed_ref[...]).astype(BF16)
    lanes = pack_ref.shape[2]
    pack_ref[...] = jnp.zeros(pack_ref.shape, BF16)
    pack_ref[0] = part[:, :lanes]
    pack_ref[1, :, : width - lanes] = part[:, lanes:]
    dense.start_pair()
    dense.scatter()
    grad_x_ref[...] = (mixed_ref[...].astype(F32) + dot_cols(mixed_ref[...], wd_ref[...])).astype(BF16)
    for n, refs in enumerate(mine):
        for k in range(2):
            pairs[2 * n + k].wait_recv()
            refs[3][k] = (refs[k][...].astype(F32) + refs[2][k].astype(F32)).astype(BF16)
    dense.gather()
    dense_out[1] = sums_ref[0, :, :width]
    for k, (at1, at3) in enumerate(((wide + half, 2 * half), (wide, 0))):
        s1_out[k] = sums_ref[0, :, at1 : at1 + ff]
        s3_out[k] = sums_ref[1, :, at3 : at3 + ff]
        down = sums_ref[1, :, at3 + half : at3 + 2 * half].astype(F32)
        s2_out[k] = jnp.transpose(down)[:ff, :].astype(BF16)
    dense.swap()
    for copy in pairs:
        copy.wait_send()
    dense.finish()
    dense_out[0, :, :lanes] = full_ref[0].reshape(width, lanes)
    dense_out[0, :, lanes:] = full_ref[1].reshape(width, lanes)[:, : width - lanes]


def solution(mesh):
    ep = mesh.shape["ep"]
    tok_spec = P(ALL_AXES, None)
    route_spec = P(None, ALL_AXES, None)
    exp_spec = P(None, "ep", None, None)
    repl_spec = P(None, None, None)

    def body(act_in, grad_out, slot_ids, gate_vals, w_dense, w_gate, w_up, w_down, ws_gate, ws_up, ws_down):
        tokens, width = act_in.shape
        ff = w_gate.shape[3]
        local = w_gate.shape[1]
        cap = 2 * tokens * 2 // (local * ep)
        wide, half = pad_lanes(width), pad_lanes(ff)
        block = (ep, cap, local * width)
        slot_rows = jnp.swapaxes(slot_ids, 1, 2)
        row = np.arange(ep * cap)
        slots_of_row = jnp.asarray(((row // cap) * local * cap + row % cap).astype(np.int32))[None, :]
        send = pltpu.VMEM(block, BF16)
        token_pads = [pltpu.VMEM((tokens, wide), BF16)] * 2
        copy_pads = [pltpu.VMEM((2 * tokens, wide), BF16)] * 2
        weights = [pltpu.VMEM((2, wide, 2 * half), BF16), pltpu.VMEM((2, half, wide), BF16)]
        accs = [pltpu.VMEM((2, wide, 2 * half), F32), pltpu.VMEM((2, half, wide), F32)]
        hidden_tmp = [pltpu.VMEM((tokens, ff), BF16)] * 3
        sems = exchange_scratch(ep, cap)
        tok = shape((tokens, width))
        blk = shape(block)
        eg = [shape((local, width, ff)), shape((local, width, ff)), shape((local, ff, width))]
        lanes = wide + 2 * half + 2 * LANE
        tiles = width // TILE

        u1, rows1, grads2, back1 = call(
            first_kernel,
            (act_in, w_dense[0], slot_rows[0], w_gate[0], w_up[0], w_down[0], grad_out, gate_vals[1], slot_rows[1]),
            (tok, blk, blk, blk),
            [send, *token_pads, send, *copy_pads, send, *weights, *sems, *sems, *sems],
            1,
        )
        x2, u2, ret2, *eg2 = call(
            middle_kernel,
            (back1, slots_of_row, slot_ids[0], gate_vals[0], u1, ws_gate[0], ws_up[0], ws_down[0], w_dense[1], slot_rows[1], grads2, w_gate[1], w_up[1], w_down[1]),
            (tok, tok, blk, *eg),
            [send, send, *token_pads, send, *weights, *accs, *sems, *sems],
            2,
        )
        grad_x2, shared1, ret1, eg_gate, eg_up, eg_down, sums = call(
            turn_kernel,
            (ret2, slots_of_row, slot_ids[1], grad_out, u2, x2, ws_gate[1], ws_up[1], ws_down[1], w_dense[1], gate_vals[0], slot_rows[0], rows1, w_gate[0], w_up[0], w_down[0], u1, ws_gate[0], ws_up[0], ws_down[0]),
            (tok, shape((tokens, width), F32), blk, *eg, shape((2, tiles, TILE, lanes))),
            [send, send, *copy_pads, send, *weights, *accs, pltpu.VMEM((tokens, width), BF16), *hidden_tmp, pltpu.VMEM((2, width, lanes), BF16), *sems, *sems, *sum_scratch(ep, width, lanes)],
            3,
        )
        last_lanes = wide // 2
        pairs = [(2, local, width, ff), (2, local, width, ff), (2, local, ff, width)]
        return call(
            last_kernel,
            (ret1, slots_of_row, slot_ids[0], grad_x2, shared1, act_in, w_dense[0], sums.reshape(2, width, lanes), eg_gate, eg_up, eg_down, *eg2),
            (tok, shape((2, width, width)), *[shape(s) for s in pairs], shape((2, width, ff)), shape((2, width, ff)), shape((2, ff, width))),
            [
                pltpu.VMEM((tokens, width), BF16),
                pltpu.VMEM((2, width, last_lanes), BF16),
                pltpu.VMEM((2, tiles, TILE, last_lanes), BF16),
                *[pltpu.VMEM(s, BF16) for s in pairs],
                pltpu.SemaphoreType.DMA((3, 2)),
                pltpu.SemaphoreType.DMA((3, 2)),
                *sum_scratch(ep, width, last_lanes),
            ],
            4,
        )

    return jax.shard_map(body, mesh=mesh, in_specs=(tok_spec, tok_spec, route_spec, route_spec, repl_spec, exp_spec, exp_spec, exp_spec, repl_spec, repl_spec, repl_spec), out_specs=(tok_spec, repl_spec, exp_spec, exp_spec, exp_spec, repl_spec, repl_spec, repl_spec), check_vma=False)
```

time: 520 us -> 437 us (0.84); the launches traced: 510 us -> 433 us
  Pallas kernels: 467 us -> 400 us
  other arithmetic: 8.88 us -> 0 us
    pallas_call x9 -> x4, Pallas kernels: 467 us -> 400 us  [call(): pl.pallas_call(kernel, out_shape=outs, in_specs=[vmem() for _ in ins], ou...]
    another operation x3 -> x0, other arithmetic: 8.88 us -> none  [the longest x2 5.62 us: body(): stacked = [jnp.stack([a, b]) for a, b in zip(eg1, eg2)]]
    pallas_call x0 -> x5, local copies, waits for them, and re-layouts: none -> 7.53 us  [call(): pl.pallas_call(kernel, out_shape=outs, in_specs=[vmem() for _ in ins], ou...]
    unnamed x59 -> x49, local copies, waits for them, and re-layouts: 23.5 us -> 18.9 us
where the time goes in v2:
time: 437 us; the launch traced here: 433 us
  Pallas kernels  400 us (92%)
  local copies, waits for them, and re-layouts  32.5 us (7%)
    pallas_call x4, Pallas kernels, call(): pl.pallas_call(kernel, out_shape=outs, in_specs=[vmem() for _ in ins], ou...  400 us
    unnamed x49, local copies, waits for them, and re-layouts  18.9 us

profile of v2, /device:TPU:1, one launch (start us, length us, event | category | flops | bytes accessed | tf_op | source)
XLA Modules:
  0.0 433.4 jit_solution(11231248425255393173)
XLA Ops:
  0.6 0.8 fusion.5
  1.4 1.3 slice_bitcast_fusion.6
  2.7 0.7 fusion.4
  3.4 0.9 copy.50
  4.4 0.9 copy.45
  5.3 0.9 copy.44
  6.3 1.0 copy.43
  7.3 0.9 copy.51
  8.2 0.9 copy.46
  9.2 0.9 copy.52
  10.1 0.9 copy.47
  11.1 0.9 slice_bitcast_fusion.4
  12.0 1.2 copy.23.x_ref
  13.1 1.2 copy.24.grad_ref
  14.3 1.0 slice_bitcast_fusion.2
  16.0 1.1 copy.48
  17.1 1.1 copy.41
  18.3 1.1 copy.49
  19.5 1.1 copy.42
  20.6 1.1 slice_bitcast_fusion
  21.7 135.3 %shard_map.179 = (bf16[768,448]{1,0:T(8,128)(2,1)}, bf16[64,24,896]{2,1,0:T(8,128)(2,1)}, bf16[64,24,896]{2,1,0:T(8,128)(2,1)}, bf16[64,24,896]{2,1,0:T(8,128)(2,1)}) custom-call(bf16[768,448]{1,0:T(8,128)(2,1)} %copy.23.x_ref, bf16[448,448]{1,0:T(8,128)(2,1)} %get-tuple-element.57.wd_ref, s32[2,768]{1,0:T(2,128)} %get-tuple-element.69.slot_row_ref, ...), custom_call_target="tpu_custom_call" | custom-call | tf_op jit(solution)/shard_map/pallas_call | solution.py:269
  157.0 88.8 %shard_map.180 = (bf16[768,448]{1,0:T(8,128)(2,1)}, bf16[768,448]{1,0:T(8,128)(2,1)}, bf16[64,24,896]{2,1,0:T(8,128)(2,1)}, bf16[2,448,304]{2,1,0:T(8,128)(2,1)}...) custom-call(bf16[64,24,896]{2,1,0:T(8,128)(2,1)} %get-tuple-element.25.back_ref, ...), custom_call_target="tpu_custom_call" | custom-call | tf_op jit(solution)/shard_map/pallas_call | solution.py:269
  245.8 133.7 %shard_map.181 = (bf16[768,448]{1,0:T(8,128)(2,1)}, f32[768,448]{1,0:T(8,128)}, bf16[64,24,896]{2,1,0:T(8,128)(2,1)}, bf16[2,448,304]{2,1,0:T(8,128)(2,1)}, bf16...) custom-call(bf16[64,24,896]{2,1,0:T(8,128)(2,1)} %get-tuple-element.28.ret2_ref, ...), custom_call_target="tpu_custom_call" | custom-call | tf_op jit(solution)/shard_map/pallas_call | solution.py:269
  379.6 41.8 %shard_map.182 = (bf16[768,448]{1,0:T(8,128)(2,1)}, bf16[2,448,448]{2,1,0:T(8,128)(2,1)}, bf16[2,2,448,304]{3,2,1,0:T(8,128)(2,1)}, bf16[2,2,448,304]{3,2,1,0:T(...) custom-call(bf16[64,24,896]{2,1,0:T(8,128)(2,1)} %get-tuple-element., ...), custom_call_target="tpu_custom_call" | custom-call | tf_op jit(solution)/shard_map/pallas_call | solution.py:269
  421.4 2.3 copy.36
  423.8 1.1 copy.39
  424.9 1.1 copy.40
  426.0 1.5 copy.37
  427.5 1.5 copy.38
  429.0 0.9 copy.56
  430.6 1.0 copy.57
  432.1 0.8 copy.58
  (36 shorter events, 2.1 us)
Async XLA Ops:
  0.6 6.6 %copy-start.12 = (bf16[2,448,304]{1,2,0:T(8,128)(2,1)S(1)}, bf16[2,448,304]{1,2,0:T(8,128)(2,1)}, u32[]{:S(2)}) copy-start(bf16[2,448,304]{1,2,0:T(8,128)(2,1)} %param.20) | copy-start | bytes 1634308
  7.2 1.9 copy-start.13
  9.2 1.9 copy-start.14
  9.2 2.8 copy-start.8
  11.1 2.1 copy-start.9
  12.0 2.3 copy-start.6
  14.3 1.6 copy-start.2
  16.0 2.3 copy-start.3
  18.3 2.3 copy-start.4
  421.4 2.4 copy-start.11
  421.4 3.5 copy-start.10
  423.8 2.2 copy-start.1
  426.0 1.5 copy-start
  427.5 1.5 copy-start.7
  429.0 1.6 copy-start.5
  430.6 1.5 copy-start.15
